TPU v7x, 128 devices: a whole 4x4x4 slice. The times are simulated.
128 devices in a mesh: band: 8 (over y, x_hi), slab: 16 (over x_lo, z, core).
Axes of the slice: x: 4 (x_hi: 2, x_lo: 2; x = x_hi * 2 + x_lo), y: 4, z: 4, core: 2. Of those that a mesh axis runs over, the one named last changes fastest.
Arguments:
- band_block: float32 [8, 2, 2, 128, 128, 128], P(None, None, None, 'band', 'slab'), may hold values from -24 to 24
- material_grid: int32 [128, 128, 128], P('slab'), may hold values from 0 to 3
- inverse_permittivity: float32 [4], replicated, may hold values from 0.077 to 1
- bloch_index: int32 [1], replicated, may hold values from 0 to 7
Outputs:
- search_block: float32 [8, 2, 2, 128, 128, 128], P(None, None, None, 'band', 'slab')
- correlation: float32 [2, 16, 16], replicated
- projected: float32 [2, 16, 16], replicated
All inputs are finite; a program needn't handle non-finite values.
Results may differ from a plain program's by a relative error of at most 0.00005.
Values sent between devices are 32-bit elements; how exact they have to be, the bound alone decides.
A program may use at most 192 MiB of HBM per device.

v0:
```python
from functools import partial
import functools
import math

import jax
import jax.numpy as jnp
from jax import lax
from jax.sharding import Mesh
from jax.sharding import PartitionSpec as P

KPOINTS = 8
BAND = ("band_0", "band_1")
SLAB = ("slab_0", "slab_1", "slab_2")
BAND_SLAB = ("band_0", "band_1", "slab_0", "slab_1", "slab_2")


HIGHEST = lax.Precision.HIGHEST


def one_axis_at_a_time(shard, axes):
    return functools.reduce(lax.psum, axes, shard)


def axis_values(length, weight, fraction, offset, extent):
    indices = offset + jnp.arange(extent, dtype=jnp.int32)
    signed = jnp.where(indices >= length // 2, indices - length, indices).astype(jnp.float32)
    return 2.0 * math.pi / length * (signed + weight * fraction)


def frame(depth_wave, height_wave, width_wave):
    depth_term = depth_wave[:, None, None]
    height_term = height_wave[None, :, None]
    width_term = width_wave[None, None, :]
    planar = jnp.sqrt(width_term * width_term + height_term * height_term)
    magnitude = jnp.sqrt(planar * planar + depth_term * depth_term)
    grid_shape = magnitude.shape
    primary = [
        jnp.broadcast_to(height_term / planar, grid_shape),
        jnp.broadcast_to(-width_term / planar, grid_shape),
        jnp.zeros(grid_shape, magnitude.dtype),
    ]
    secondary = [
        width_term * depth_term / (magnitude * planar),
        height_term * depth_term / (magnitude * planar),
        -planar / magnitude,
    ]
    return (primary, secondary, magnitude)


def curl_field(block, primary, secondary, magnitude):
    first_comp = block[:, 0]
    second_comp = block[:, 1]
    parts = [
        magnitude * (first_comp * secondary[component] - second_comp * primary[component])
        for component in range(3)
    ]
    return jnp.stack(parts, axis=1).reshape((-1,) + first_comp.shape[1:])


def project_back(spectrum, primary, secondary, magnitude, band_count):
    grouped = spectrum.reshape((band_count, 3) + spectrum.shape[1:])
    along_second = (
        grouped[:, 0] * secondary[0] + grouped[:, 1] * secondary[1] + grouped[:, 2] * secondary[2]
    )
    along_primary = (
        grouped[:, 0] * primary[0] + grouped[:, 1] * primary[1] + grouped[:, 2] * primary[2]
    )
    return jnp.stack([magnitude * along_second, -magnitude * along_primary], axis=1)


def transform(values, target, direction):
    length = values.shape[target]
    indices = jnp.arange(length, dtype=jnp.int32)
    products = indices[:, None] * indices[None, :] % length
    angles = 2.0 * math.pi / length * products.astype(jnp.float32)
    cosine = jnp.cos(angles)
    sine_table = direction * jnp.sin(angles)
    letters = "abc"
    source = letters[target - 2]
    formula = "i" + letters + "," + source + "w" + "->" + "i" + letters.replace(source, "w")
    contract = partial(jnp.einsum, formula, precision=HIGHEST)
    real_part = values[:, 0]
    imaginary = values[:, 1]
    new_real = contract(real_part, cosine) - contract(imaginary, sine_table)
    new_imag = contract(real_part, sine_table) + contract(imaginary, cosine)
    return jnp.stack([new_real, new_imag], axis=1)


def cell_values(material_grid, inverse_permittivity, grid_cells):
    inverse_cells = jnp.zeros(material_grid.shape, jnp.float32)
    for material in range(inverse_permittivity.shape[0]):
        inverse_cells = inverse_cells + jnp.where(
            material_grid == material, inverse_permittivity[material], 0.0
        )
    return inverse_cells / grid_cells


def gram_parts(left, right):
    left_real = left[:, :, 0].reshape(left.shape[0], -1)
    left_imag = left[:, :, 1].reshape(left.shape[0], -1)
    right_real = right[:, :, 0].reshape(right.shape[0], -1)
    right_imag = right[:, :, 1].reshape(right.shape[0], -1)
    inner_product = partial(jnp.einsum, "km,jm->kj", precision=HIGHEST)
    real_sum = inner_product(left_real, right_real) + inner_product(left_imag, right_imag)
    imag_sum = inner_product(left_real, right_imag) - inner_product(left_imag, right_real)
    return (real_sum, imag_sum)


def shards(band_block, material_grid, inverse_permittivity, bloch_index):
    band_groups = lax.axis_size(BAND)
    slab_count = lax.axis_size(SLAB)
    band_count = band_block.shape[0]
    depth_share = band_block.shape[3]
    row_share = band_block.shape[4]
    line_length = band_block.shape[5]
    full_depth = depth_share * band_groups
    full_rows = row_share * slab_count
    grid_cells = full_depth * full_rows * line_length
    fraction = (bloch_index[0].astype(jnp.float32) + 1.0) / KPOINTS
    row_offset = lax.axis_index(SLAB) * row_share
    depth_offset = lax.axis_index(BAND) * depth_share
    width_wave = axis_values(line_length, 0.5, fraction, 0, line_length)
    row_wave = axis_values(full_rows, 0.35, fraction, row_offset, row_share)
    point_frame = frame(
        axis_values(full_depth, 0.2, fraction, depth_offset, depth_share), row_wave, width_wave
    )
    inverse_cells = cell_values(material_grid, inverse_permittivity, grid_cells)

    def slab_operator(points):
        gathered = lax.all_to_all(points, BAND, split_axis=0, concat_axis=3, tiled=True)
        primary, secondary, magnitude = frame(
            axis_values(full_depth, 0.2, fraction, 0, full_depth), row_wave, width_wave
        )
        curled = curl_field(gathered, primary, secondary, magnitude)
        spectrum = transform(transform(curled, 4, 1.0), 2, 1.0)
        spatial = (
            transform(
                lax.all_to_all(spectrum, SLAB, split_axis=2, concat_axis=3, tiled=True), 3, 1.0
            )
            * inverse_cells[None, None]
        )
        returned = lax.all_to_all(
            transform(spatial, 3, -1.0), SLAB, split_axis=3, concat_axis=2, tiled=True
        )
        finished = transform(transform(returned, 2, -1.0), 4, -1.0)
        local_image = project_back(finished, primary, secondary, magnitude, gathered.shape[0])
        return lax.all_to_all(local_image, BAND, split_axis=3, concat_axis=0, tiled=True)

    def apply_operator(points):
        return slab_operator(points)

    image = apply_operator(band_block)
    correlation_real, correlation_imag = gram_parts(band_block, band_block)
    cross_real, cross_imag = gram_parts(band_block, image)
    correlation_real, correlation_imag, cross_real, cross_imag = (
        one_axis_at_a_time(correlation_real, BAND_SLAB),
        one_axis_at_a_time(correlation_imag, BAND_SLAB),
        one_axis_at_a_time(cross_real, BAND_SLAB),
        one_axis_at_a_time(cross_imag, BAND_SLAB),
    )
    correlation_real = correlation_real / grid_cells
    correlation_imag = correlation_imag / grid_cells
    cross_real = cross_real / grid_cells
    cross_imag = cross_imag / grid_cells
    system = jnp.concatenate(
        [
            jnp.concatenate([correlation_real, -correlation_imag], 1),
            jnp.concatenate([correlation_imag, correlation_real], 1),
        ],
        0,
    )
    right_side = jnp.concatenate([cross_real, cross_imag], 0)
    factor = jnp.linalg.cholesky(system)
    solution = jax.scipy.linalg.cho_solve((factor, True), right_side)
    mixing_real = solution[:band_count]
    mixing_imag = solution[band_count:]
    block_real = band_block[:, :, 0]
    block_imag = band_block[:, :, 1]
    combine = partial(jnp.einsum, "iabcd,ij->jabcd", precision=HIGHEST)
    residual_real = image[:, :, 0] - (
        combine(block_real, mixing_real) - combine(block_imag, mixing_imag)
    )
    residual_imag = image[:, :, 1] - (
        combine(block_real, mixing_imag) + combine(block_imag, mixing_real)
    )
    magnitude = point_frame[2]
    search_block = jnp.stack([residual_real, residual_imag], axis=2) / (magnitude * magnitude + 1.0)
    search_image = apply_operator(search_block)
    stacked = jnp.concatenate([band_block, search_block], 0)
    joint_real, joint_imag = gram_parts(stacked, search_block)
    image_real, image_imag = gram_parts(stacked, search_image)
    back_real, back_imag = gram_parts(search_block, image)
    joint_real, joint_imag, image_real, image_imag, back_real, back_imag = (
        one_axis_at_a_time(joint_real, BAND_SLAB),
        one_axis_at_a_time(joint_imag, BAND_SLAB),
        one_axis_at_a_time(image_real, BAND_SLAB),
        one_axis_at_a_time(image_imag, BAND_SLAB),
        one_axis_at_a_time(back_real, BAND_SLAB),
        one_axis_at_a_time(back_imag, BAND_SLAB),
    )
    joint_real = joint_real / grid_cells
    joint_imag = joint_imag / grid_cells
    image_real = image_real / grid_cells
    image_imag = image_imag / grid_cells
    back_real = back_real / grid_cells
    back_imag = back_imag / grid_cells
    upper_real = jnp.concatenate([correlation_real, joint_real[:band_count]], 1)
    lower_real = jnp.concatenate([joint_real[:band_count].T, joint_real[band_count:]], 1)
    upper_imag = jnp.concatenate([correlation_imag, joint_imag[:band_count]], 1)
    lower_imag = jnp.concatenate([-joint_imag[:band_count].T, joint_imag[band_count:]], 1)
    correlation = jnp.stack(
        [
            jnp.concatenate([upper_real, lower_real], 0),
            jnp.concatenate([upper_imag, lower_imag], 0),
        ],
        0,
    )
    top_real = jnp.concatenate([cross_real, image_real[:band_count]], 1)
    bottom_real = jnp.concatenate([back_real, image_real[band_count:]], 1)
    top_imag = jnp.concatenate([cross_imag, image_imag[:band_count]], 1)
    bottom_imag = jnp.concatenate([back_imag, image_imag[band_count:]], 1)
    projected = jnp.stack(
        [jnp.concatenate([top_real, bottom_real], 0), jnp.concatenate([top_imag, bottom_imag], 0)],
        0,
    )
    return (search_block, correlation, projected)


def solution(mesh):
    finer = Mesh(
        mesh.devices.reshape(4, 2, 2, 4, 2), ("band_0", "band_1", "slab_0", "slab_1", "slab_2")
    )
    placed = (P(None, None, None, BAND, SLAB, None), P(SLAB, None, None), P(), P())
    return jax.shard_map(
        shards,
        mesh=finer,
        in_specs=placed,
        out_specs=(P(None, None, None, BAND, SLAB, None), P(), P()),
        check_vma=False,
    )
```

profile of v0, /device:TPU:1, one launch (start us, length us, event | category | flops | bytes accessed | tf_op | source)
XLA Modules:
  0.0 597.2 jit_solution(14836860329177111146)
XLA Ops:
  0.6 7.5 %all-to-all-start = ((f32[8,2,2,16,8,128]{5,4,3,2,1,0:T(8,128)}), f32[8,2,2,16,8,128]{5,4,3,2,1,0:T(8,128)}, u32[]{:S(2)}, u32[]{:S(2)}) async-start(f32[8,2,2,16,8,128]{5,4,3,2,1,0:T(8,128)} %param.4), calls=%async_computation | async-start | bytes 4194304 | tf_op jit(solution)/shard_map/all_to_all | solution.py:130
  10.3 25.5 %all-to-all-done = f32[8,2,2,16,8,128]{5,4,3,2,1,0:T(8,128)} async-done(((f32[8,2,2,16,8,128]{5,4,3,2,1,0:T(8,128)}), f32[8,2,2,16,8,128]{5,4,3,2,1,0:T(8,128)}, u32[]{:S(2)}, u32[]{:S(2)}) %all-to-all-start) | async-done | bytes 2097184 | tf_op jit(solution)/shard_map/all_to_all | solution.py:130
  52.8 3.5 copy.133
  56.4 7.3 %all-to-all-start.1 = ((f32[3,2,128,8,128]{4,3,0,1,2:T(8,128)}), f32[3,2,128,8,128]{4,3,0,1,2:T(8,128)}, u32[]{:S(2)}, u32[]{:S(2)}) async-start(f32[3,2,128,8,128]{4,3,0,1,2:T(8,128)} %copy.133), calls=%async_computation.1 | async-start | bytes 6291456 | tf_op jit(solution)/shard_map/all_to_all | solution.py:138
  64.4 3.6 add_multiply_fusion.4
  67.9 36.4 %all-to-all-done.1 = f32[3,2,128,8,128]{4,3,0,1,2:T(8,128)} async-done(((f32[3,2,128,8,128]{4,3,0,1,2:T(8,128)}), f32[3,2,128,8,128]{4,3,0,1,2:T(8,128)}, u32[]{:S(2)}, u32[]{:S(2)}) %all-to-all-start.1) | async-done | bytes 3145760 | tf_op jit(solution)/shard_map/all_to_all | solution.py:138
  117.6 13.5 %subtract_bitcast_fusion.5 = f32[3,1,8,128,128]{4,3,2,0,1:T(8,128)S(1)} fusion(f32[128,3,8,128]{3,0,2,1:T(8,128)S(1)} %fusion.32, f32[3,2,8,128,128]{4,3,2,0,1:T(8,128)S(1)} %maximum_multiply_fusion), kind=kOutput, calls=%fused_computation.68 | convolution fusion | flops 604618752 | bytes 4718592 | tf_op jit(solution)/shard_map/iabc,bw->iawc/dot_general | solution.py:84
  134.9 47.6 %all_to_all.144 = f32[3,2,8,128,128]{4,2,0,1,3:T(8,128)S(1)} all-to-all(f32[3,2,8,128,128]{4,2,0,1,3:T(8,128)S(1)} %copy.143), channel_id=1, replica_groups=mesh['band_0'=4,'band_1'=2,'slab_0'=2,'slab_1'=4,'slab_2'=2] {'slab_0','..., dimensions={3} | all-to-all | bytes 6291456 | tf_op jit(solution)/shard_map/all_to_all | solution.py:142
  199.4 2.5 copy.149
  201.9 4.4 all-to-all-start.3
  206.3 2.8 copy.152
  211.5 2.4 convolution_bitcast_fusion.16
  214.0 2.4 fusion.51
  218.8 14.8 %all-to-all-done.3 = f32[1,2,2,128,8,128]{5,4,1,2,0,3:T(8,128)} async-done(((f32[1,2,2,128,8,128]{5,4,1,2,0,3:T(8,128)}), f32[1,2,2,128,8,128]{5,4,1,2,0,3:T(8,128)}, u32[]{:S(2)}, u32[]{:S(2)}) %all-to-all-start.3) | async-done | bytes 2097184 | tf_op jit(solution)/shard_map/all_to_all | solution.py:147
  233.6 2.8 copy.308
  236.4 2.5 convolution_bitcast_fusion.14
  238.9 2.5 convolution_bitcast_fusion.12
  241.4 2.7 fusion.54
  244.1 2.5 fusion.56
  246.6 11.4 %all-reduce.3 = (f32[8,8]{0,1:T(8,128)S(1)}, f32[8,8]{0,1:T(8,128)S(1)}, f32[8,8]{0,1:T(8,128)S(1)}, f32[8,8]{0,1:T(8,128)S(1)}) all-reduce(f32[8,8]{0,1:T(8,128)S(1)} %fusion.51, f32[8,8]{0,1:T(8,128)S(1)} %fusion.52, f32[8,8]{0,1:T(8,128)S(1)} %fusion.56, ...), channel_id=1, replica_groups=mesh['band_0'=4,'band_1'=2,'slab_0'=2,'slab_1'=4,'slab_2'=2] {'band_0'}, use_global_device_ids=true, to_apply=%region_0.1 | all-reduce | flops 256 | bytes 2048 | tf_op jit(solution)/shard_map/psum | solution.py:21
  258.0 8.6 %all-reduce.9 = (f32[8,8]{0,1:T(8,128)S(1)}, f32[8,8]{0,1:T(8,128)S(1)}, f32[8,8]{0,1:T(8,128)S(1)}, f32[8,8]{0,1:T(8,128)S(1)}) all-reduce(f32[8,8]{0,1:T(8,128)S(1)} %get-tuple-element.28, f32[8,8]{0,1:T(8,128)S(1)} %get-tuple-element.29, ...), channel_id=1, replica_groups=mesh['band_0'=4,'band_1'=2,'slab_0'=2,'slab_1'=4,'slab_2'=2] {'band_1'}, use_global_device_ids=true, to_apply=%region_1.2 | all-reduce | flops 256 | bytes 2048 | tf_op jit(solution)/shard_map/psum | solution.py:21
  266.6 6.0 %all-reduce.7 = (f32[8,8]{0,1:T(8,128)S(1)}, f32[8,8]{0,1:T(8,128)S(1)}, f32[8,8]{0,1:T(8,128)S(1)}, f32[8,8]{0,1:T(8,128)S(1)}) all-reduce(f32[8,8]{0,1:T(8,128)S(1)} %get-tuple-element.58, f32[8,8]{0,1:T(8,128)S(1)} %get-tuple-element.59, ...), channel_id=1, replica_groups=mesh['band_0'=4,'band_1'=2,'slab_0'=2,'slab_1'=4,'slab_2'=2] {'slab_0'}, use_global_device_ids=true, to_apply=%region_2.3 | all-reduce | flops 256 | bytes 2048 | tf_op jit(solution)/shard_map/psum | solution.py:21
  272.6 11.9 %all-reduce.1 = (f32[8,8]{0,1:T(8,128)S(1)}, f32[8,8]{0,1:T(8,128)S(1)}, f32[8,8]{0,1:T(8,128)S(1)}, f32[8,8]{0,1:T(8,128)S(1)}) all-reduce(f32[8,8]{0,1:T(8,128)S(1)} %get-tuple-element.48, f32[8,8]{0,1:T(8,128)S(1)} %get-tuple-element.49, ...), channel_id=1, replica_groups=mesh['band_0'=4,'band_1'=2,'slab_0'=2,'slab_1'=4,'slab_2'=2] {'slab_1'}, use_global_device_ids=true, to_apply=%region_3.4 | all-reduce | flops 256 | bytes 2048 | tf_op jit(solution)/shard_map/psum | solution.py:21
  284.5 14.8 %all-reduce.5 = (f32[8,8]{0,1:T(8,128)S(1)}, f32[8,8]{0,1:T(8,128)S(1)}, f32[8,8]{0,1:T(8,128)S(1)}, f32[8,8]{0,1:T(8,128)S(1)}) all-reduce(f32[8,8]{0,1:T(8,128)S(1)} %get-tuple-element.18, f32[8,8]{0,1:T(8,128)S(1)} %get-tuple-element.19, ...), channel_id=1, replica_groups=mesh['band_0'=4,'band_1'=2,'slab_0'=2,'slab_1'=4,'slab_2'=2] {'slab_2'}, use_global_device_ids=true, to_apply=%region_4.5 | all-reduce | flops 256 | bytes 2048 | tf_op jit(solution)/shard_map/psum | solution.py:21
  310.5 32.6 %all_to_all.145 = f32[8,2,2,16,8,128]{5,4,3,1,2,0:T(8,128)S(1)} all-to-all(f32[8,2,2,16,8,128]{5,4,3,1,2,0:T(8,128)S(1)} %copy.163), channel_id=1, replica_groups=mesh['band_0'=4,'band_1'=2,'slab_0'=2,'slab_1'=4,'slab_2'=2] {'band_0','..., dimensions={0} | all-to-all | bytes 4194304 | tf_op jit(solution)/shard_map/all_to_all | solution.py:130
  361.3 41.9 %all_to_all.146 = f32[3,2,128,8,128]{4,3,0,1,2:T(8,128)S(1)} all-to-all(f32[3,2,128,8,128]{4,3,0,1,2:T(8,128)S(1)} %copy.169), channel_id=1, replica_groups=mesh['band_0'=4,'band_1'=2,'slab_0'=2,'slab_1'=4,'slab_2'=2] {'slab_0','..., dimensions={2} | all-to-all | bytes 6291456 | tf_op jit(solution)/shard_map/all_to_all | solution.py:138
  419.0 3.5 copy.179
  422.5 5.5 all-to-all-start.6
  428.0 3.5 copy.192
  436.2 31.6 %all-to-all-done.6 = f32[3,2,8,128,128]{4,2,0,1,3:T(8,128)} async-done(((f32[3,2,8,128,128]{4,2,0,1,3:T(8,128)}), f32[3,2,8,128,128]{4,2,0,1,3:T(8,128)}, u32[]{:S(2)}, u32[]{:S(2)}) %all-to-all-start.6) | async-done | bytes 3145760 | tf_op jit(solution)/shard_map/all_to_all | solution.py:142
  486.3 2.6 copy.185
  488.8 4.6 all-to-all-start.7
  495.6 2.6 convolution_bitcast_fusion.11
  498.2 2.6 convolution_bitcast_fusion.9
  500.9 2.5 fusion.57
  505.8 2.7 fusion.50
  508.5 2.6 fusion.49
  511.1 9.9 %all-to-all-done.7 = f32[1,2,2,128,8,128]{5,4,1,2,0,3:T(8,128)} async-done(((f32[1,2,2,128,8,128]{5,4,1,2,0,3:T(8,128)}), f32[1,2,2,128,8,128]{5,4,1,2,0,3:T(8,128)}, u32[]{:S(2)}, u32[]{:S(2)}) %all-to-all-start.7) | async-done | bytes 2097184 | tf_op jit(solution)/shard_map/all_to_all | solution.py:147
  521.0 3.2 copy.307
  524.2 2.7 convolution_bitcast_fusion.7
  526.9 2.7 convolution_bitcast_fusion.3
  529.6 2.7 fusion.48
  532.2 2.6 fusion.47
  534.9 12.1 %all-reduce.2 = (f32[16,8]{0,1:T(8,128)S(1)}, f32[16,8]{0,1:T(8,128)S(1)}, f32[16,8]{0,1:T(8,128)S(1)}, f32[8,8]{0,1:T(8,128)S(1)}, f32[16,8]{0,1:T(8,128)S(1)}, /*index=5*/f32[8,8]{0,1:T(8,128)S(1)}) all-reduce(f32[16,8]{0,1:T(8,128)S(1)} %fusion.49, ...), channel_id=1, replica_groups=mesh['band_0'=4,'band_1'=2,'slab_0'=2,'slab_1'=4,'slab_2'=2] {'band_0'}, use_global_device_ids=true, to_apply=%region_27.28 | all-reduce | flops 640 | bytes 5120 | tf_op jit(solution)/shard_map/psum | solution.py:21
  547.0 7.7 %all-reduce.8 = (f32[16,8]{0,1:T(8,128)S(1)}, f32[16,8]{0,1:T(8,128)S(1)}, f32[16,8]{0,1:T(8,128)S(1)}, f32[8,8]{0,1:T(8,128)S(1)}, f32[16,8]{0,1:T(8,128)S(1)}, /*index=5*/f32[8,8]{0,1:T(8,128)S(1)}) all-reduce(f32[16,8]{0,1:T(8,128)S(1)} %get-tuple-element.22, ...), channel_id=1, replica_groups=mesh['band_0'=4,'band_1'=2,'slab_0'=2,'slab_1'=4,'slab_2'=2] {'band_1'}, use_global_device_ids=true, to_apply=%region_28.29 | all-reduce | flops 640 | bytes 5120 | tf_op jit(solution)/shard_map/psum | solution.py:21
  554.7 5.4 all-reduce.6
  560.1 19.3 %all-reduce = (f32[16,8]{0,1:T(8,128)S(1)}, f32[16,8]{0,1:T(8,128)S(1)}, f32[16,8]{0,1:T(8,128)S(1)}, f32[8,8]{0,1:T(8,128)S(1)}, f32[16,8]{0,1:T(8,128)S(1)}, /*index=5*/f32[8,8]{0,1:T(8,128)S(1)}) all-reduce(f32[16,8]{0,1:T(8,128)S(1)} %get-tuple-element.42, ...), channel_id=1, replica_groups=mesh['band_0'=4,'band_1'=2,'slab_0'=2,'slab_1'=4,'slab_2'=2] {'slab_1'}, use_global_device_ids=true, to_apply=%region_30.31 | all-reduce | flops 640 | bytes 5120 | tf_op jit(solution)/shard_map/psum | solution.py:21
  579.4 15.2 %all-reduce.4 = (f32[16,8]{0,1:T(8,128)S(1)}, f32[16,8]{0,1:T(8,128)S(1)}, f32[16,8]{0,1:T(8,128)S(1)}, f32[8,8]{0,1:T(8,128)S(1)}, f32[16,8]{0,1:T(8,128)S(1)}, /*index=5*/f32[8,8]{0,1:T(8,128)S(1)}) all-reduce(f32[16,8]{0,1:T(8,128)S(1)} %get-tuple-element.12, ...), channel_id=1, replica_groups=mesh['band_0'=4,'band_1'=2,'slab_0'=2,'slab_1'=4,'slab_2'=2] {'slab_2'}, use_global_device_ids=true, to_apply=%region_31.32 | all-reduce | flops 640 | bytes 5120 | tf_op jit(solution)/shard_map/psum | solution.py:21
  (176 shorter events, 132.3 us)
Async XLA Ops:
  0.6 35.2 %all-to-all-start = ((f32[8,2,2,16,8,128]{5,4,3,2,1,0:T(8,128)}), f32[8,2,2,16,8,128]{5,4,3,2,1,0:T(8,128)}, u32[]{:S(2)}, u32[]{:S(2)}) async-start(f32[8,2,2,16,8,128]{5,4,3,2,1,0:T(8,128)} %param.4), calls=%async_computation | async-start | bytes 4194304 | tf_op jit(solution)/shard_map/all_to_all | solution.py:130
  10.3 27.5 %copy-start.14 = (f32[128,8,128]{2,0,1:T(8,128)}, f32[128,8,128]{2,0,1:T(8,128)S(1)}, u32[]{:S(2)}) copy-start(f32[128,8,128]{2,0,1:T(8,128)S(1)} %get-tuple-element.82) | copy-start | bytes 1572868
  10.3 187.1 %copy-start.11 = (f32[128,8,128]{2,0,1:T(8,128)}, f32[128,8,128]{2,0,1:T(8,128)S(1)}, u32[]{:S(2)}) copy-start(f32[128,8,128]{2,0,1:T(8,128)S(1)} %get-tuple-element.81) | copy-start | bytes 1572868
  56.4 7.3 %copy-start.23 = (f32[4]{0:T(128)S(1)}, f32[4]{0:T(128)}, u32[]{:S(2)}) copy-start(f32[4]{0:T(128)} %param.6) | copy-start | bytes 52
  56.4 8.0 %copy-start.22 = (s32[8,128,128]{2,1,0:T(8,128)S(1)}, s32[8,128,128]{2,1,0:T(8,128)}, u32[]{:S(2)}) copy-start(s32[8,128,128]{2,1,0:T(8,128)} %param.5) | copy-start | bytes 1572868
  56.4 48.0 %all-to-all-start.1 = ((f32[3,2,128,8,128]{4,3,0,1,2:T(8,128)}), f32[3,2,128,8,128]{4,3,0,1,2:T(8,128)}, u32[]{:S(2)}, u32[]{:S(2)}) async-start(f32[3,2,128,8,128]{4,3,0,1,2:T(8,128)} %copy.133), calls=%async_computation.1 | async-start | bytes 6291456 | tf_op jit(solution)/shard_map/all_to_all | solution.py:138
  112.0 1.8 copy-start.20
  197.2 1.0 copy-start.15
  197.2 1.2 copy-start.18
  201.9 31.6 %all-to-all-start.3 = ((f32[1,2,2,128,8,128]{5,4,1,2,0,3:T(8,128)}), f32[1,2,2,128,8,128]{5,4,1,2,0,3:T(8,128)}, u32[]{:S(2)}, u32[]{:S(2)}) async-start(f32[1,2,2,128,8,128]{5,4,1,2,0,3:T(8,128)} %copy.149), calls=%async_computation.3 | async-start | bytes 4194304 | tf_op jit(solution)/shard_map/all_to_all | solution.py:147
  236.4 7.7 %copy-start.3 = (f32[1,2,2,8,16,8,128]{6,3,5,4,1,2,0:T(8,128)}, f32[1,2,2,8,16,8,128]{6,3,5,4,1,2,0:T(8,128)S(1)}, u32[]{:S(2)}) copy-start(f32[1,2,2,8,16,8,128]{6,3,5,4,1,2,0:T(8,128)S(1)} %copy.308) | copy-start | bytes 6291460
  305.0 1.6 copy-start.4
  309.1 1.4 copy-start
  343.1 1.0 copy-start.12
  343.1 1.2 copy-start.16
  408.9 1.9 copy-start.21
  422.5 45.3 %all-to-all-start.6 = ((f32[3,2,8,128,128]{4,2,0,1,3:T(8,128)}), f32[3,2,8,128,128]{4,2,0,1,3:T(8,128)}, u32[]{:S(2)}, u32[]{:S(2)}) async-start(f32[3,2,8,128,128]{4,2,0,1,3:T(8,128)} %copy.179), calls=%async_computation.6 | async-start | bytes 6291456 | tf_op jit(solution)/shard_map/all_to_all | solution.py:142
  428.0 3.5 copy-start.1
  428.0 3.5 copy-start.5
  484.0 1.0 copy-start.13
  484.0 1.2 copy-start.17
  484.0 1.3 copy-start.19
  488.8 32.2 %all-to-all-start.7 = ((f32[1,2,2,128,8,128]{5,4,1,2,0,3:T(8,128)}), f32[1,2,2,128,8,128]{5,4,1,2,0,3:T(8,128)}, u32[]{:S(2)}, u32[]{:S(2)}) async-start(f32[1,2,2,128,8,128]{5,4,1,2,0,3:T(8,128)} %copy.185), calls=%async_computation.7 | async-start | bytes 4194304 | tf_op jit(solution)/shard_map/all_to_all | solution.py:147
  493.4 2.2 copy-start.2
  495.5 10.3 %copy-start.9 = (f32[16,2,16,8,128]{4,0,3,2,1:T(8,128)}, f32[16,2,16,8,128]{4,0,3,2,1:T(8,128)S(1)}, u32[]{:S(2)}) copy-start(f32[16,2,16,8,128]{4,0,3,2,1:T(8,128)S(1)} %get-tuple-element.65) | copy-start | bytes 6291460
  495.5 13.0 %copy-start.7 = (f32[16,2,16,8,128]{4,0,3,2,1:T(8,128)}, f32[16,2,16,8,128]{4,0,3,2,1:T(8,128)S(1)}, u32[]{:S(2)}) copy-start(f32[16,2,16,8,128]{4,0,3,2,1:T(8,128)S(1)} %get-tuple-element.64) | copy-start | bytes 6291460
  498.2 2.6 copy-start.6
  521.0 3.2 copy-start.10
  526.9 2.7 copy-start.8
where the time goes:
time: 607 us; the launch traced here: 597 us
  blocking collectives  235 us (39%)
  matrix products  151 us (25%)
  waiting for transfers between devices  118 us (19%)
  local copies, waits for them, and re-layouts  43.2 us (7%)
  starting transfers between devices  29.2 us (5%)
  other arithmetic  18.1 us (3%)
    psum x10, blocking collectives, one_axis_at_a_time(): return functools.reduce(lax.psum, axes, shard)  113 us
    dot_general x24, matrix products, transform(): new_real = contract(real_part, cosine) - contract(imaginary, sine_table)  54.1 us
    all_to_all x1, blocking collectives, slab_operator(): lax.all_to_all(transform(spatial, 3, -1.0), SLAB, split_axis=3, concat_ax...  47.6 us
    dot_general x24, matrix products, transform(): new_imag = contract(real_part, sine_table) + contract(imaginary, cosine)  42.1 us
    all_to_all x1, blocking collectives, slab_operator(): lax.all_to_all(spectrum, SLAB, split_axis=2, concat_axis=3, tiled=True)  41.9 us
    all_to_all x1, waiting for transfers between devices, slab_operator(): lax.all_to_all(spectrum, SLAB, split_axis=2, concat_axis=3, tiled=True)  36.4 us
    all_to_all x1, blocking collectives, slab_operator(): lax.all_to_all(points, BAND, split_axis=0, concat_axis=3, tiled=True)  32.6 us
    all_to_all x1, waiting for transfers between devices, slab_operator(): lax.all_to_all(transform(spatial, 3, -1.0), SLAB, split_axis=3, concat_ax...  31.6 us
  transfers between devices with their start and end apart: 5, of which 5 were waited for; matrix products, arithmetic and copies ran while one was open for 7% of the time, Pallas kernels for 0%

commit v1 on v0

v1 whole, which is shorter than its diff:
```python
import functools
import math

import jax
import jax.numpy as jnp
import numpy as np
from jax import lax
from jax.experimental import pallas as pl
from jax.experimental.pallas import tpu as pltpu
from jax.sharding import Mesh
from jax.sharding import PartitionSpec as P

KPOINTS = 8
N = 128
CELLS = N * N * N
BANDS = 8
BAND = ("band_0", "band_1")
SLAB = ("slab_0", "slab_1", "slab_2")
HIGHEST = lax.Precision.HIGHEST
F32 = jnp.float32
BF16 = jnp.bfloat16


def _rot(angle):
    c, s = np.cos(angle), np.sin(angle)
    return np.stack([np.stack([c, -s]), np.stack([s, c])])


def _halves(table):
    high = table.astype(BF16)
    low = (table - high.astype(np.float64)).astype(BF16)
    return high, low


def _left(table):
    high, low = _halves(table)
    return np.concatenate([high, high, low], 1)


def _right(table):
    high, low = _halves(table)
    return np.concatenate([high, high, low], 0)


def tables():
    tau = 2.0 * math.pi
    i128, i16, i8 = np.arange(128), np.arange(16), np.arange(8)
    r = _rot(tau / 128 * (i128[:, None] * i128[None, :] % 128))
    ta = r.reshape(2, 2, 16, 8, 128).transpose(2, 0, 3, 1, 4).reshape(256, 256)
    r = _rot(tau / 8 * (i8[:, None] * i8[None, :] % 8))
    kz = np.einsum("abzs,xy->azxsby", r, np.eye(8)).reshape(128, 128)
    r = _rot(tau / 16 * (i16[:, None] * i16[None, :] % 16))
    wz = np.einsum("abos,xy->bsxaoy", r, np.eye(8)).reshape(256, 256)
    r = _rot(tau / 16 * (i16[:, None] * i16[None, :] % 16)).reshape(2, 2, 16, 2, 8)
    ky = np.einsum("abolq,xy->aoxqlby", r, np.eye(8)).reshape(256, 256)
    r = _rot(tau / 8 * (i8[:, None] * i8[None, :] % 8))
    wy = np.einsum("abos,xy->bxsayo", r, np.eye(16)).reshape(256, 256)
    lane = np.arange(128)
    az = tau / 128 * ((np.arange(64) // 8)[:, None] * (lane // 8)[None, :])
    ay = tau / 128 * ((np.arange(128) // 8)[:, None] * (lane % 8)[None, :])
    twz = np.stack([np.cos(az), np.sin(az)]).astype(np.float32)
    twy = np.stack([np.cos(ay), np.sin(ay)]).astype(np.float32)
    gather = np.zeros((128, 16), np.float32)
    for band in range(8):
        for part in range(2):
            gather[(band * 2 + part) * 8 : (band * 2 + part + 1) * 8, part * 8 + band] = 1.0
    turn = np.zeros((16, 16), np.float32)
    turn[:8, 8:] = np.eye(8)
    turn[8:, :8] = -np.eye(8)
    turned = gather @ turn.T
    collect = np.concatenate([gather.T, turned.T], 0)
    place = np.zeros((4, 2, 128, 128), np.float32)
    for slot in range(4):
        place[slot, 0, :, slot * 16 : slot * 16 + 16] = gather
        place[slot, 1, :, slot * 16 : slot * 16 + 16] = turned
    spread = np.zeros((128, 128), np.float32)
    spread[16:32] = gather.T
    same = (lane[:, None] % 8 == lane[None, :] % 8).astype(np.float32)
    return dict(
        ta=_left(ta), tat=_left(ta.T), kz=_left(kz), kzt=_left(kz.T), ky=_left(ky), kyt=_left(ky.T),
        wz=_right(wz), wzt=_right(wz.T), wy=_right(wy), wyt=_right(wy.T),
        twz=twz, twy=twy, collect=collect, place=place, spread=spread, gather=gather, same=same,
    )


NAMES = ("ta", "tat", "kz", "kzt", "ky", "kyt", "wz", "wzt", "wy", "wyt", "twz", "twy",
         "collect", "place", "spread", "gather", "same")


def parts(x):
    high = x.astype(BF16)
    low = (x - high.astype(F32)).astype(BF16)
    return high, low


def rows_dot(table3, x):
    high, low = parts(x)
    return jnp.dot(table3[...], jnp.concatenate([high, low, high], 0), preferred_element_type=F32)


def lanes_dot(x, table3):
    high, low = parts(x)
    return jnp.dot(jnp.concatenate([high, low, high], 1), table3[...], preferred_element_type=F32)


def exact_dot(x, y):
    return jnp.dot(x, y, precision=HIGHEST, preferred_element_type=F32)


def turn_by(re, im, cosine, sine):
    return re * cosine - im * sine, re * sine + im * cosine


def turn_back(re, im, cosine, sine):
    return re * cosine + im * sine, im * cosine - re * sine


def cut(x, size, axis=1):
    return [lax.slice_in_dim(x, k, k + size, axis=axis) for k in range(0, x.shape[axis], size)]


def z_forward(tab, blocks):
    mixed = rows_dot(tab["kz"], blocks)
    cosine, sine = tab["twz"][0], tab["twz"][1]
    pairs = [turn_by(b[:64], b[64:], cosine, sine) for b in cut(mixed, 128)]
    both = jnp.concatenate(
        [jnp.concatenate([a for a, _ in pairs], 0), jnp.concatenate([b for _, b in pairs], 0)], 1
    )
    return lanes_dot(both, tab["wz"])


def z_back(tab, both):
    mixed = lanes_dot(both, tab["wzt"])
    cosine, sine = tab["twz"][0], tab["twz"][1]
    blocks = []
    for b in cut(mixed, 64, 0):
        re, im = turn_back(b[:, :128], b[:, 128:], cosine, sine)
        blocks.append(jnp.concatenate([re, im], 0))
    return rows_dot(tab["kzt"], jnp.concatenate(blocks, 1))


def y_forward(tab, blocks):
    mixed = rows_dot(tab["ky"], blocks)
    cosine, sine = tab["twy"][0], tab["twy"][1]
    pairs = [turn_by(b[:128], b[128:], cosine, sine) for b in cut(mixed, 128)]
    both = jnp.concatenate(
        [jnp.concatenate([a for a, _ in pairs], 0), jnp.concatenate([b for _, b in pairs], 0)], 1
    )
    return lanes_dot(both, tab["wy"])


def y_back(tab, both):
    mixed = lanes_dot(both, tab["wyt"])
    cosine, sine = tab["twy"][0], tab["twy"][1]
    blocks = []
    for b in cut(mixed, 128, 0):
        re, im = turn_back(b[:, :128], b[:, 128:], cosine, sine)
        blocks.append(jnp.concatenate([re, im], 0))
    return rows_dot(tab["kyt"], jnp.concatenate(blocks, 1))


def axis_values(length, weight, fraction, indices):
    signed = jnp.where(indices >= length // 2, indices - length, indices).astype(F32)
    return 2.0 * math.pi / length * (signed + weight * fraction)


def kernel(bloch_ref, band_ref, cell_ref, *refs):
    tab = dict(zip(NAMES, refs[: len(NAMES)]))
    (out_ref, first_ref, second_ref, coef, xt, image, search, fields,
     s_a, r_a, s_b, r_b, s_c, r_c, s_d, r_d, s_small, r_one, r_two,
     send_x, recv_x, send_small, recv_small) = refs[len(NAMES):]
    y_me, xh_me, xl_me = (lax.axis_index(a) for a in ("band_0", "band_1", "slab_0"))
    z_me, c_me = lax.axis_index("slab_1"), lax.axis_index("slab_2")
    p_me = xl_me * 8 + y_me * 2 + xh_me
    q_me = z_me * 2 + c_me
    x_me = xh_me * 2 + xl_me

    def wide_peer(k):
        y = (y_me + k // 4) % 4
        x = (x_me + k % 4) % 4
        return {"band_0": y, "band_1": x // 2, "slab_0": x % 2}, (x % 2) * 8 + y * 2 + x // 2

    def deep_peer(k):
        z = (z_me + k // 2) % 4
        c = (c_me + k % 2) % 2
        return {"slab_1": z, "slab_2": c}, z * 2 + c

    barrier = pltpu.get_barrier_semaphore()
    for k in range(1, 16):
        pl.semaphore_signal(barrier, inc=1, device_id=wide_peer(k)[0], device_id_type=pl.DeviceIdType.MESH)
    for k in range(1, 8):
        pl.semaphore_signal(barrier, inc=1, device_id=deep_peer(k)[0], device_id_type=pl.DeviceIdType.MESH)
    pl.semaphore_wait(barrier, 22)

    def send(kind, t, source, target, peers, count, me):
        for k in range(1, count):
            device, slot = peers(k)
            pltpu.make_async_remote_copy(
                src_ref=source.at[slot], dst_ref=target.at[me],
                send_sem=send_x.at[kind, t], recv_sem=recv_x.at[kind, t],
                device_id=device, device_id_type=pl.DeviceIdType.MESH,
            ).start()
        target[me] = source[me]

    def descriptor(kind, t, source, target, count):
        return pltpu.make_async_remote_copy(
            src_ref=source.at[pl.ds(0, count - 1)], dst_ref=target.at[pl.ds(0, count - 1)],
            send_sem=send_x.at[kind, t], recv_sem=recv_x.at[kind, t],
            device_id=deep_peer(1)[0], device_id_type=pl.DeviceIdType.MESH,
        )

    def start_sum(slot):
        for k in range(1, 16):
            device, _ = wide_peer(k)
            pltpu.make_async_remote_copy(
                src_ref=s_small.at[slot, 0], dst_ref=r_one.at[slot, p_me],
                send_sem=send_small.at[slot, 0], recv_sem=recv_small.at[slot, 0],
                device_id=device, device_id_type=pl.DeviceIdType.MESH,
            ).start()
        r_one[slot, p_me] = s_small[slot, 0]

    def small_wait(slot, step, target, count):
        return pltpu.make_async_remote_copy(
            src_ref=target.at[slot, pl.ds(0, count - 1)], dst_ref=target.at[slot, pl.ds(0, count - 1)],
            send_sem=send_small.at[slot, step], recv_sem=recv_small.at[slot, step],
            device_id=deep_peer(1)[0], device_id_type=pl.DeviceIdType.MESH,
        )

    def middle_sum(slot):
        small_wait(slot, 0, r_one, 16).wait_recv()
        s_small[slot, 1] = jnp.sum(r_one[slot], axis=0)
        for k in range(1, 8):
            device, _ = deep_peer(k)
            pltpu.make_async_remote_copy(
                src_ref=s_small.at[slot, 1], dst_ref=r_two.at[slot, q_me],
                send_sem=send_small.at[slot, 1], recv_sem=recv_small.at[slot, 1],
                device_id=device, device_id_type=pl.DeviceIdType.MESH,
            ).start()
        r_two[slot, q_me] = s_small[slot, 1]

    def finish_sum(slot):
        small_wait(slot, 1, r_two, 8).wait_recv()
        return jnp.sum(r_two[slot], axis=0)

    fraction = (bloch_ref[0].astype(F32) + 1.0) / KPOINTS
    row = lax.broadcasted_iota(jnp.int32, (N, N), 0)
    lane = lax.broadcasted_iota(jnp.int32, (N, N), 1)
    qx = axis_values(N, 0.5, fraction, row)
    qz = axis_values(N, 0.2, fraction, (y_me * 2 + xh_me) * 16 + lane // 8)
    qy = axis_values(N, 0.35, fraction, (xl_me * 8 + q_me) * 8 + lane % 8)
    planar = jnp.sqrt(qx * qx + qy * qy)
    magnitude = jnp.sqrt(planar * planar + qz * qz)
    coef[0] = magnitude * (qx * qz / (magnitude * planar))
    coef[1] = magnitude * (qy * qz / (magnitude * planar))
    coef[2] = magnitude * (-planar / magnitude)
    coef[3] = magnitude * (qy / planar)
    coef[4] = magnitude * (-qx / planar)
    coef[5] = 1.0 / (magnitude * magnitude + 1.0)

    def curl_and_send(kind, t, block):
        columns = []
        for c in range(3):
            halves = []
            for part in range(2):
                term = coef[c] * block[part]
                if c < 2:
                    term = term - coef[3 + c] * block[2 + part]
                halves.append(term)
            columns.append(jnp.concatenate(halves, 0))
        spread_x = rows_dot(tab["ta"][...], jnp.concatenate(columns, 1))
        for c in range(3):
            s_a[kind // 4, t, :, c] = spread_x[:, c * N : (c + 1) * N].reshape(16, 2, 8, N)
        send(kind, t, s_a.at[kind // 4, t], r_a.at[kind // 4, t], wide_peer, 16, p_me)

    def z_stage(kind, t):
        op = kind // 4
        descriptor(kind - 1, t, s_a.at[op, t], r_a.at[op, t], 16).wait_recv()
        blocks = [r_a[op, t, pl.ds(xlo * 8, 8), c].reshape(N, N) for c in range(3) for xlo in range(2)]
        both = z_forward(tab, jnp.concatenate(blocks, 1))
        for k in range(6):
            for part in range(2):
                s_b[op, t, :, k, part] = both[k * 64 : (k + 1) * 64, part * N : (part + 1) * N].reshape(8, 8, N)
        send(kind, t, s_b.at[op, t], r_b.at[op, t], deep_peer, 8, q_me)

    def y_stage(kind, t):
        op = kind // 4
        descriptor(kind, t, s_b.at[op, t], r_b.at[op, t], 8).wait_recv()
        blocks = [r_b[op, t, :, pl.ds(2 * c, 2)].reshape(256, N) for c in range(3)]
        both = y_forward(tab, jnp.concatenate(blocks, 1))
        for c in range(3):
            for part in range(2):
                fields[t, c, part] = both[c * N : (c + 1) * N, part * N : (part + 1) * N].reshape(16, 8, N)
        return both

    def first_y_stage(t):
        both = y_stage(1, t)
        cell = cell_ref[...]
        cell = jnp.concatenate([jnp.concatenate([cell, cell], 1)] * 3, 0)
        back = y_back(tab, both * cell)
        for c in range(3):
            s_c[t, :, pl.ds(2 * c, 2)] = back[:, c * N : (c + 1) * N].reshape(8, 2, 2, 8, N)
        send(2, t, s_c.at[t], r_c.at[t], deep_peer, 8, q_me)

    def z_back_stage(t):
        descriptor(2, t, s_c.at[t], r_c.at[t], 8).wait_recv()
        rows = [
            jnp.concatenate([r_c[t, :, k, part].reshape(64, N) for part in range(2)], 1) for k in range(6)
        ]
        back = z_back(tab, jnp.concatenate(rows, 0))
        for c in range(3):
            for xlo in range(2):
                k = 2 * c + xlo
                s_d[t, pl.ds(xlo * 8, 8), c] = back[:, k * N : (k + 1) * N].reshape(8, 2, 8, N)
        send(3, t, s_d.at[t], r_d.at[t], wide_peer, 16, p_me)

    def x_back_stage(t):
        descriptor(3, t, s_d.at[t], r_d.at[t], 16).wait_recv()
        columns = [r_d[t, :, c].reshape(256, N) for c in range(3)]
        back = rows_dot(tab["tat"][...], jnp.concatenate(columns, 1))
        for part in range(2):
            g = [back[part * N : (part + 1) * N, c * N : (c + 1) * N] for c in range(3)]
            image[t, 0, part] = (g[0] * coef[0] + g[1] * coef[1] + g[2] * coef[2]).reshape(16, 8, N)
            image[t, 1, part] = (-(g[0] * coef[3] + g[1] * coef[4])).reshape(16, 8, N)

    def gram(left, right, groups, slot, scale=None):
        def body(g, total):
            comp, m0 = g // 2, (g % 2) * 8
            left_cols = [left[:, comp, :, m0 + m].reshape(N, N) for m in range(8)]
            if scale is None:
                right_cols = left_cols if right is left else [
                    right[:, comp, :, m0 + m].reshape(N, N) for m in range(8)
                ]
            else:
                right_cols = []
                for m in range(8):
                    weight = scale[pl.ds(pl.multiple_of((m0 + m) * 8, 8), 8), :]
                    right_cols.append((right[:, comp, :, m0 + m] * weight[None, None]).reshape(N, N))
            lh, ll = parts(jnp.concatenate(left_cols, 1))
            rh, rl = parts(jnp.concatenate(right_cols, 1))
            return total + lax.dot_general(
                jnp.concatenate([lh, ll, lh], 1), jnp.concatenate([rh, rh, rl], 1),
                (((1,), (1,)), ((), ())), preferred_element_type=F32,
            )
        total = lax.fori_loop(0, groups, body, jnp.zeros((N, N), F32))
        folded = exact_dot(tab["collect"][...], total * tab["same"][...])
        return exact_dot(folded[:16], tab["place"][slot, 0]) + exact_dot(folded[16:], tab["place"][slot, 1])

    def first_step(t, carry):
        @pl.when(t < 8)
        def _():
            for comp in range(2):
                for part in range(2):
                    xt[t, comp, part] = band_ref[t, comp, part].reshape(N, N).T.reshape(16, 8, N)
            curl_and_send(0, t, [xt[t, c, r].reshape(N, N) for c in range(2) for r in range(2)])

        @pl.when((t >= 1) & (t < 9))
        def _():
            z_stage(1, t - 1)

        @pl.when((t >= 2) & (t < 10))
        def _():
            first_y_stage(t - 2)

        @pl.when((t >= 3) & (t < 11))
        def _():
            z_back_stage(t - 3)

        @pl.when((t >= 4) & (t < 12))
        def _():
            x_back_stage(t - 4)

        @pl.when(t == 9)
        def _():
            s_small[0, 0] = gram(xt, xt, 4, 0) + gram(fields, fields, 6, 1, cell_ref)
            start_sum(0)

        @pl.when(t == 10)
        def _():
            middle_sum(0)

        return carry

    lax.fori_loop(0, 12, first_step, 0)

    system = finish_sum(0)
    first_ref[...] = system
    rows16 = lax.broadcasted_iota(jnp.int32, (16, N), 0)
    for k in range(16):
        pivot = system[k : k + 1] / system[k : k + 1, k : k + 1]
        system = jnp.where(rows16 == k, pivot, system - system[:, k : k + 1] * pivot)
    wide = exact_dot(system, tab["spread"][...])
    mixing = exact_dot(tab["gather"][...], wide).T * tab["same"][...]
    mix_high, mix_low = parts(mixing)
    mixing = jnp.concatenate([mix_high, mix_high, mix_low], 1)

    def residual_step(g, carry):
        comp, m0 = g // 2, (g % 2) * 8
        columns = jnp.concatenate([xt[:, comp, :, m0 + m].reshape(N, N) for m in range(8)], 1)
        mixed = rows_dot(mixing, columns)
        for m in range(8):
            scale = coef[5, pl.ds(pl.multiple_of((m0 + m) * 8, 8), 8), :]
            search[:, comp, :, m0 + m] = (
                image[:, comp, :, m0 + m] - mixed[:, m * N : (m + 1) * N].reshape(8, 2, 8, N)
            ) * scale[None, None]
        return carry

    lax.fori_loop(0, 4, residual_step, 0)

    def second_step(t, carry):
        @pl.when(t < 8)
        def _():
            curl_and_send(4, t, [search[t, c, r].reshape(N, N) for c in range(2) for r in range(2)])
            for comp in range(2):
                for part in range(2):
                    out_ref[t, comp, part] = search[t, comp, part].reshape(N, N).T.reshape(16, 8, N)

        @pl.when((t >= 1) & (t < 9))
        def _():
            z_stage(5, t - 1)

        @pl.when((t >= 2) & (t < 10))
        def _():
            y_stage(5, t - 2)

        @pl.when(t == 8)
        def _():
            s_small[1, 0] = gram(xt, search, 4, 0) + gram(search, search, 4, 1) + gram(search, image, 4, 2)

        return carry

    lax.fori_loop(0, 10, second_step, 0)
    s_small[1, 0] = s_small[1, 0] + gram(fields, fields, 6, 3, cell_ref)
    start_sum(1)
    middle_sum(1)
    second_ref[...] = finish_sum(1)

    def drain(t, carry):
        descriptor(0, t, s_a.at[0, t], r_a.at[0, t], 16).wait_send()
        descriptor(1, t, s_b.at[0, t], r_b.at[0, t], 8).wait_send()
        descriptor(2, t, s_c.at[t], r_c.at[t], 8).wait_send()
        descriptor(3, t, s_d.at[t], r_d.at[t], 16).wait_send()
        descriptor(4, t, s_a.at[1, t], r_a.at[1, t], 16).wait_send()
        descriptor(5, t, s_b.at[1, t], r_b.at[1, t], 8).wait_send()
        return carry

    lax.fori_loop(0, 8, drain, 0)
    for slot in range(2):
        small_wait(slot, 0, r_one, 16).wait_send()
        small_wait(slot, 1, r_two, 8).wait_send()


def shards(band_block, material_grid, inverse_permittivity, bloch_index):
    cells = jnp.zeros(material_grid.shape, F32)
    for material in range(inverse_permittivity.shape[0]):
        cells = cells + jnp.where(material_grid == material, inverse_permittivity[material], 0.0)
    cells = cells / CELLS
    block = lax.axis_index(BAND)
    cells = cells.reshape(8, N, 2, 8, 8)
    cells = lax.dynamic_index_in_dim(cells, block, 3, keepdims=False)
    cells = cells.transpose(2, 0, 1, 3).reshape(16, N, 8)
    cells = lax.all_to_all(cells, SLAB, split_axis=0, concat_axis=0, tiled=True)
    cells = cells.reshape(16, 8, 16, 8).transpose(2, 3, 0, 1).reshape(N, N)

    table = tables()
    vmem = pl.BlockSpec(memory_space=pltpu.VMEM)
    search, first, second = pl.pallas_call(
        kernel,
        out_shape=(
            jax.ShapeDtypeStruct(band_block.shape, F32),
            jax.ShapeDtypeStruct((16, N), F32),
            jax.ShapeDtypeStruct((16, N), F32),
        ),
        in_specs=[pl.BlockSpec(memory_space=pltpu.SMEM)] + [vmem] * (2 + len(NAMES)),
        out_specs=(vmem, vmem, vmem),
        scratch_shapes=[
            pltpu.VMEM((6, N, N), F32),
            pltpu.VMEM((8, 2, 2, 16, 8, N), F32),
            pltpu.VMEM((8, 2, 2, 16, 8, N), F32),
            pltpu.VMEM((8, 2, 2, 16, 8, N), F32),
            pltpu.VMEM((8, 3, 2, 16, 8, N), F32),
            pltpu.VMEM((2, 8, 16, 3, 2, 8, N), F32),
            pltpu.VMEM((2, 8, 16, 3, 2, 8, N), F32),
            pltpu.VMEM((2, 8, 8, 6, 2, 8, N), F32),
            pltpu.VMEM((2, 8, 8, 6, 2, 8, N), F32),
            pltpu.VMEM((8, 8, 6, 2, 8, N), F32),
            pltpu.VMEM((8, 8, 6, 2, 8, N), F32),
            pltpu.VMEM((8, 16, 3, 2, 8, N), F32),
            pltpu.VMEM((8, 16, 3, 2, 8, N), F32),
            pltpu.VMEM((2, 2, 16, N), F32),
            pltpu.VMEM((2, 16, 16, N), F32),
            pltpu.VMEM((2, 8, 16, N), F32),
            pltpu.SemaphoreType.DMA((6, 8)),
            pltpu.SemaphoreType.DMA((6, 8)),
            pltpu.SemaphoreType.DMA((2, 2)),
            pltpu.SemaphoreType.DMA((2, 2)),
        ],
        compiler_params=pltpu.CompilerParams(
            collective_id=0, has_side_effects=True, vmem_limit_bytes=63 * 1024 * 1024
        ),
    )(bloch_index, band_block, cells, *[jnp.asarray(table[name]) for name in NAMES])

    first = first / CELLS
    second = second / CELLS

    def pair(tile, slot):
        return tile[:8, slot * 16 : slot * 16 + 8], tile[:8, slot * 16 + 8 : slot * 16 + 16]

    def joined(corner, right, below, last):
        return jnp.concatenate(
            [jnp.concatenate([corner, right], 1), jnp.concatenate([below, last], 1)], 0
        )

    s_re, s_im = pair(first, 0)
    h_re, h_im = pair(first, 1)
    xs_re, xs_im = pair(second, 0)
    ss_re, ss_im = pair(second, 1)
    b_re, b_im = pair(second, 2)
    p_re, p_im = pair(second, 3)
    correlation = jnp.stack([joined(s_re, xs_re, xs_re.T, ss_re), joined(s_im, xs_im, -xs_im.T, ss_im)])
    projected = jnp.stack([joined(h_re, b_re.T, b_re, p_re), joined(h_im, -b_im.T, b_im, p_im)])
    return search, correlation, projected


def solution(mesh):
    finer = Mesh(
        mesh.devices.reshape(4, 2, 2, 4, 2), ("band_0", "band_1", "slab_0", "slab_1", "slab_2")
    )
    placed = (P(None, None, None, BAND, SLAB, None), P(SLAB, None, None), P(), P())
    return jax.shard_map(
        shards,
        mesh=finer,
        in_specs=placed,
        out_specs=(P(None, None, None, BAND, SLAB, None), P(), P()),
        check_vma=False,
    )
```

time: 607 us -> 202 us (0.33); the launches traced: 597 us -> 202 us
  blocking collectives: 235 us -> 0 us
  Pallas kernels: 0 us -> 172 us
  matrix products: 151 us -> 0 us
  waiting for transfers between devices: 118 us -> 5.17 us
  local copies, waits for them, and re-layouts: 43.2 us -> 10.6 us
  starting transfers between devices: 29.2 us -> 7.75 us
  other arithmetic: 18.1 us -> 4.42 us
    pallas_call x0 -> x1, Pallas kernels: none -> 172 us  [shards(): pl.pallas_call(kernel, out_shape=(jax.ShapeDtypeStruct(band_block.shape,...]
    dot_general x72 -> x0, matrix products: 151 us -> none  [the longest x24 54.1 us: transform(): new_real = contract(real_part, cosine) - contract(imaginary, sine_table)]
    all_to_all x3 -> x0, blocking collectives: 122 us -> none  [the longest x1 47.6 us: slab_operator(): lax.all_to_all(transform(spatial, 3, -1.0), SLAB, split_axis=3, concat_ax...]
    all_to_all x5 -> x1, waiting for transfers between devices: 118 us -> 5.17 us  [shards(): cells = lax.all_to_all(cells, SLAB, split_axis=0, concat_axis=0, tiled=True)]
    psum x10 -> x0, blocking collectives: 113 us -> none  [one_axis_at_a_time(): return functools.reduce(lax.psum, axes, shard)]
    all_to_all x5 -> x1, starting transfers between devices: 29.2 us -> 7.75 us  [shards(): cells = lax.all_to_all(cells, SLAB, split_axis=0, concat_axis=0, tiled=True)]
    another operation x6 -> x0, local copies, waits for them, and re-layouts: 15.8 us -> none  [the longest x4 10.7 us: transform(): return jnp.stack([new_real, new_imag], axis=1)]
    all_to_all x8 -> x0, local copies, waits for them, and re-layouts: 13.7 us -> none  [the longest x2 6.01 us: slab_operator(): lax.all_to_all(local_image, BAND, split_axis=3, concat_axis=0, tiled=True)]
  transfers between devices with their start and end apart: 5 -> 1, of which waited for: 5 -> 1; matrix products, arithmetic and copies ran while one was open for 7% -> 0% of each run, Pallas kernels for 0% -> 0%
where the time goes in v1:
time: 202 us
  Pallas kernels  172 us (85%)
  local copies, waits for them, and re-layouts  10.6 us (5%)
  starting transfers between devices  7.75 us (4%)
  waiting for transfers between devices  5.17 us (3%)
  other arithmetic  4.42 us (2%)
    pallas_call x1, Pallas kernels, shards(): pl.pallas_call(kernel, out_shape=(jax.ShapeDtypeStruct(band_block.shape,...  172 us
    all_to_all x1, starting transfers between devices, shards(): cells = lax.all_to_all(cells, SLAB, split_axis=0, concat_axis=0, tiled=True)  7.75 us
    unnamed x6, local copies, waits for them, and re-layouts  5.26 us
    all_to_all x1, waiting for transfers between devices, shards(): cells = lax.all_to_all(cells, SLAB, split_axis=0, concat_axis=0, tiled=True)  5.17 us
  transfers between devices with their start and end apart: 1, of which 1 were waited for; matrix products, arithmetic and copies ran while one was open for 0% of the time, Pallas kernels for 0%

profile of v1, /device:TPU:1, one launch (start us, length us, event | category | flops | bytes accessed | tf_op | source)
XLA Modules:
  0.0 201.5 jit_solution(4879827005668279874)
XLA Ops:
  0.6 1.4 fusion.1
  2.0 1.2 copy.65
  3.3 2.7 %add_multiply_fusion = f32[8,128,128]{1,2,0:T(8,128)S(1)} fusion(s32[8,128,128]{1,2,0:T(8,128)S(1)} %copy.65, f32[]{:T(128)} %bitcast.3, f32[]{:T(128)} %bitcast.2, f32[]{:T(128)} %bitcast.1, f32[]{:T(128)} %bitcast), kind=kLoop, calls=%fused_computation | loop fusion | flops 1572864 | bytes 1048592 | tf_op jit(solution)/shard_map/div | solution.py:456
  6.0 0.6 copy.69
  6.7 7.7 %all-to-all-start = ((f32[16,128,8]{1,2,0:T(8,128)}), f32[16,128,8]{1,2,0:T(8,128)S(1)}, u32[]{:S(2)}, u32[]{:S(2)}) async-start(f32[16,128,8]{1,2,0:T(8,128)} %bitcast.7), calls=%async_computation | async-start | bytes 131072 | tf_op jit(solution)/shard_map/all_to_all | solution.py:461
  15.0 5.2 %all-to-all-done = f32[16,128,8]{1,2,0:T(8,128)S(1)} async-done(((f32[16,128,8]{1,2,0:T(8,128)}), f32[16,128,8]{1,2,0:T(8,128)S(1)}, u32[]{:S(2)}, u32[]{:S(2)}) %all-to-all-start) | async-done | bytes 65568 | tf_op jit(solution)/shard_map/all_to_all | solution.py:461
  20.2 0.2 reshape.20
  20.4 0.9 copy.70
  21.3 1.1 reshape.21.cell_ref
  22.4 172.3 %shard_map.220 = (f32[8,2,2,16,8,128]{5,4,3,2,1,0:T(8,128)}, f32[16,128]{1,0:T(8,128)}, f32[16,128]{1,0:T(8,128)}) custom-call(s32[1]{0:T(128)S(6)} %copy.85.bloch_ref, f32[8,2,2,16,8,128]{5,4,3,2,1,0:T(8,128)} %band_ref.1, f32[128,128]{1,0:T(8,128)} %reshape.21.cell_ref, bf16[256,768]{1,0:T(8,128)(2,1)} %constant.68.clone.refs_0_, ...), custom_call_target="tpu_custom_call" | custom-call | tf_op jit(solution)/shard_map/pallas_call | solution.py:466
  194.7 0.7 broadcast_multiply_fusion.1
  195.4 0.1 slice_bitcast_fusion
  195.5 0.1 copy.82
  195.5 0.1 copy.76
  195.6 0.1 copy.83
  195.7 0.8 copy.71
  196.5 0.1 copy.78
  196.6 0.1 copy.79
  196.6 0.1 copy.81
  196.7 0.1 pad_maximum_fusion.4
  196.8 0.1 copy.75
  196.9 0.1 maximum_bitcast_fusion
  197.0 0.7 copy.80
  197.6 0.1 maximum_bitcast_fusion.2
  197.7 0.1 maximum_bitcast_fusion.3
  197.8 0.6 pad_maximum_fusion.1
  198.4 3.1 %copy.86 = f32[8,2,2,16,8,128]{5,4,3,2,1,0:T(8,128)} copy(f32[8,2,2,16,8,128]{5,4,3,2,1,0:T(8,128)} %get-tuple-element.48) | data formatting | bytes 4194304
  (5 shorter events, 0.0 us)
Async XLA Ops:
  6.7 13.6 %all-to-all-start = ((f32[16,128,8]{1,2,0:T(8,128)}), f32[16,128,8]{1,2,0:T(8,128)S(1)}, u32[]{:S(2)}, u32[]{:S(2)}) async-start(f32[16,128,8]{1,2,0:T(8,128)} %bitcast.7), calls=%async_computation | async-start | bytes 131072 | tf_op jit(solution)/shard_map/all_to_all | solution.py:461

commit v2 on v1

v2 whole, which is shorter than its diff:
```python
import functools
import math

import jax
import jax.numpy as jnp
import numpy as np
from jax import lax
from jax.experimental import pallas as pl
from jax.experimental.pallas import tpu as pltpu
from jax.sharding import Mesh
from jax.sharding import PartitionSpec as P

KPOINTS = 8
N = 128
CELLS = N * N * N
BANDS = 8
BAND = ("band_0", "band_1")
SLAB = ("slab_0", "slab_1", "slab_2")
HIGHEST = lax.Precision.HIGHEST
F32 = jnp.float32
BF16 = jnp.bfloat16


def _rot(angle):
    c, s = np.cos(angle), np.sin(angle)
    return np.stack([np.stack([c, -s]), np.stack([s, c])])


def _halves(table):
    high = table.astype(BF16)
    low = (table - high.astype(np.float64)).astype(BF16)
    return high, low


def _left(table):
    high, low = _halves(table)
    return np.concatenate([high, low], 1)


def _right(table):
    high, low = _halves(table)
    return np.concatenate([high, low], 0)


def tables():
    tau = 2.0 * math.pi
    i128, i16, i8 = np.arange(128), np.arange(16), np.arange(8)
    r = _rot(tau / 128 * (i128[:, None] * i128[None, :] % 128))
    ta = r.reshape(2, 2, 16, 8, 128).transpose(2, 0, 3, 1, 4).reshape(256, 256)
    r = _rot(tau / 8 * (i8[:, None] * i8[None, :] % 8))
    kz = np.einsum("abzs,xy->azxsby", r, np.eye(8)).reshape(128, 128)
    r = _rot(tau / 16 * (i16[:, None] * i16[None, :] % 16))
    wz = np.einsum("abos,xy->bsxaoy", r, np.eye(8)).reshape(256, 256)
    r = _rot(tau / 16 * (i16[:, None] * i16[None, :] % 16)).reshape(2, 2, 16, 2, 8)
    ky = np.einsum("abolq,xy->aoxqlby", r, np.eye(8)).reshape(256, 256)
    r = _rot(tau / 8 * (i8[:, None] * i8[None, :] % 8))
    wy = np.einsum("abos,xy->bxsayo", r, np.eye(16)).reshape(256, 256)
    lane = np.arange(128)
    az = tau / 128 * ((np.arange(64) // 8)[:, None] * (lane // 8)[None, :])
    ay = tau / 128 * ((np.arange(128) // 8)[:, None] * (lane % 8)[None, :])
    twz = np.stack([np.cos(az), np.sin(az)]).astype(np.float32)
    twy = np.stack([np.cos(ay), np.sin(ay)]).astype(np.float32)
    gather = np.zeros((128, 16), np.float32)
    for band in range(8):
        for part in range(2):
            gather[(band * 2 + part) * 8 : (band * 2 + part + 1) * 8, part * 8 + band] = 1.0
    turn = np.zeros((16, 16), np.float32)
    turn[:8, 8:] = np.eye(8)
    turn[8:, :8] = -np.eye(8)
    turned = gather @ turn.T
    collect = np.concatenate([gather.T, turned.T], 0)
    place = np.zeros((2, 128, 128), np.float32)
    place[0, :, :16] = gather
    place[1, :, :16] = turned
    spread = np.zeros((128, 128), np.float32)
    spread[16:32] = gather.T
    order = np.zeros((128, 128), np.float32)
    order[lane, lane % 16 * 8 + lane // 16] = 1.0
    return dict(
        ta=_left(ta), tat=_left(ta.T), kz=_left(kz), kzt=_left(kz.T), ky=_left(ky), kyt=_left(ky.T),
        wz=_right(wz), wzt=_right(wz.T), wy=_right(wy), wyt=_right(wy.T),
        twz=twz, twy=twy, collect=collect, place=place, spread=spread, gather=gather, order=order.astype(BF16),
    )


NAMES = ("ta", "tat", "kz", "kzt", "ky", "kyt", "wz", "wzt", "wy", "wyt", "twz", "twy",
         "collect", "place", "spread", "gather", "order")


def parts(x):
    high = x.astype(BF16)
    low = (x - high.astype(F32)).astype(BF16)
    return high, low


def rows_dot(table, x):
    high, low = parts(x)
    k = x.shape[0]
    return jnp.dot(
        jnp.concatenate([table[:, :k], table[:, :k], table[:, k:]], 1),
        jnp.concatenate([high, low, high], 0),
        preferred_element_type=F32,
    )


def lanes_dot(x, table):
    high, low = parts(x)
    k = x.shape[1]
    return jnp.dot(
        jnp.concatenate([high, low, high], 1),
        jnp.concatenate([table[:k], table[:k], table[k:]], 0),
        preferred_element_type=F32,
    )


def exact_dot(x, y):
    return jnp.dot(x, y, precision=HIGHEST, preferred_element_type=F32)


def turn_by(re, im, cosine, sine):
    return re * cosine - im * sine, re * sine + im * cosine


def turn_back(re, im, cosine, sine):
    return re * cosine + im * sine, im * cosine - re * sine


def cut(x, size, axis=1):
    return [lax.slice_in_dim(x, k, k + size, axis=axis) for k in range(0, x.shape[axis], size)]


def z_forward(tab, blocks):
    mixed = rows_dot(tab["kz"], blocks)
    cosine, sine = tab["twz"][0], tab["twz"][1]
    pairs = [turn_by(b[:64], b[64:], cosine, sine) for b in cut(mixed, 128)]
    both = jnp.concatenate(
        [jnp.concatenate([a for a, _ in pairs], 0), jnp.concatenate([b for _, b in pairs], 0)], 1
    )
    return lanes_dot(both, tab["wz"])


def z_back(tab, both):
    mixed = lanes_dot(both, tab["wzt"])
    cosine, sine = tab["twz"][0], tab["twz"][1]
    blocks = []
    for b in cut(mixed, 64, 0):
        re, im = turn_back(b[:, :128], b[:, 128:], cosine, sine)
        blocks.append(jnp.concatenate([re, im], 0))
    return rows_dot(tab["kzt"], jnp.concatenate(blocks, 1))


def y_forward(tab, blocks):
    mixed = rows_dot(tab["ky"], blocks)
    cosine, sine = tab["twy"][0], tab["twy"][1]
    pairs = [turn_by(b[:128], b[128:], cosine, sine) for b in cut(mixed, 128)]
    both = jnp.concatenate(
        [jnp.concatenate([a for a, _ in pairs], 0), jnp.concatenate([b for _, b in pairs], 0)], 1
    )
    return lanes_dot(both, tab["wy"])


def y_back(tab, both):
    mixed = lanes_dot(both, tab["wyt"])
    cosine, sine = tab["twy"][0], tab["twy"][1]
    blocks = []
    for b in cut(mixed, 128, 0):
        re, im = turn_back(b[:, :128], b[:, 128:], cosine, sine)
        blocks.append(jnp.concatenate([re, im], 0))
    return rows_dot(tab["kyt"], jnp.concatenate(blocks, 1))


def axis_values(length, weight, fraction, indices):
    signed = jnp.where(indices >= length // 2, indices - length, indices).astype(F32)
    return 2.0 * math.pi / length * (signed + weight * fraction)


LAG_BACK = 7
LAG_NEXT = 11
MESH_ID = pl.DeviceIdType.MESH


def kernel(bloch_ref, weight_ref, band_hbm, material_hbm, *refs):
    count = len(NAMES)
    table_hbm = refs[:count]
    (out_hbm, corr_ref, proj_ref, coef, band_in, material, cell, xt, image, search, out_stage, fields,
     s_a, r_a, s_b, r_b, s_c, r_c, s_d, r_d, s_cell, r_cell, s_small, r_one, r_two, first_sum, mixing,
     send_x, recv_x, send_small, recv_small, cell_sem, in_sem, table_sem, out_sem) = refs[count : -count]
    tab = dict(zip(NAMES, refs[-count:]))
    y_me, xh_me, xl_me = (lax.axis_index(a) for a in ("band_0", "band_1", "slab_0"))
    z_me, c_me = lax.axis_index("slab_1"), lax.axis_index("slab_2")
    zb_me = y_me * 2 + xh_me
    p_me = xl_me * 8 + zb_me
    q_me = z_me * 2 + c_me
    x_me = xh_me * 2 + xl_me

    def wide_peer(k):
        y = (y_me + k // 4) % 4
        x = (x_me + k % 4) % 4
        return {"band_0": y, "band_1": x // 2, "slab_0": x % 2}, (x % 2) * 8 + y * 2 + x // 2

    def deep_peer(k):
        z = (z_me + k // 2) % 4
        c = (c_me + k % 2) % 2
        return {"slab_1": z, "slab_2": c}, z * 2 + c

    def slab_peer(k):
        xl = (xl_me + k // 8) % 2
        z = (z_me + k // 2 % 4) % 4
        c = (c_me + k % 2) % 2
        return {"slab_0": xl, "slab_1": z, "slab_2": c}, xl, z * 2 + c

    def band_copy(t):
        return pltpu.make_async_copy(band_hbm.at[t], band_in.at[t], in_sem.at[t])

    def table_copy(k):
        return pltpu.make_async_copy(table_hbm[k], tab[NAMES[k]], table_sem.at[k])

    material_copy = pltpu.make_async_copy(material_hbm, material, cell_sem.at[2])
    band_copy(0).start()
    table_copy(0).start()
    for t in range(1, 8):
        band_copy(t).start()
    for k in range(1, count):
        table_copy(k).start()
    material_copy.start()

    barrier = pltpu.get_barrier_semaphore()
    for k in range(1, 16):
        pl.semaphore_signal(barrier, inc=1, device_id=wide_peer(k)[0], device_id_type=MESH_ID)
    for k in range(1, 8):
        pl.semaphore_signal(barrier, inc=1, device_id=deep_peer(k)[0], device_id_type=MESH_ID)
    for k in range(9, 16):
        pl.semaphore_signal(barrier, inc=1, device_id=slab_peer(k)[0], device_id_type=MESH_ID)

    fraction = (bloch_ref[0].astype(F32) + 1.0) / KPOINTS
    row = lax.broadcasted_iota(jnp.int32, (N, N), 0)
    lane = lax.broadcasted_iota(jnp.int32, (N, N), 1)
    qx = axis_values(N, 0.5, fraction, row)
    qz = axis_values(N, 0.2, fraction, zb_me * 16 + lane // 8)
    qy = axis_values(N, 0.35, fraction, (xl_me * 8 + q_me) * 8 + lane % 8)
    planar = jnp.sqrt(qx * qx + qy * qy)
    magnitude = jnp.sqrt(planar * planar + qz * qz)
    coef[0] = magnitude * (qx * qz / (magnitude * planar))
    coef[1] = magnitude * (qy * qz / (magnitude * planar))
    coef[2] = magnitude * (-planar / magnitude)
    coef[3] = magnitude * (qy / planar)
    coef[4] = magnitude * (-qx / planar)
    coef[5] = 1.0 / (magnitude * magnitude + 1.0)
    pl.semaphore_wait(barrier, 29)
    table_copy(0).wait()

    def send(kind, t, source, target, peers, number, me):
        for k in range(1, number):
            device, slot = peers(k)
            pltpu.make_async_remote_copy(
                src_ref=source.at[slot], dst_ref=target.at[me],
                send_sem=send_x.at[kind, t], recv_sem=recv_x.at[kind, t],
                device_id=device, device_id_type=MESH_ID,
            ).start()
        target[me] = source[me]

    def descriptor(kind, t, source, target, number):
        return pltpu.make_async_remote_copy(
            src_ref=source.at[pl.ds(0, number - 1)], dst_ref=target.at[pl.ds(0, number - 1)],
            send_sem=send_x.at[kind, t], recv_sem=recv_x.at[kind, t],
            device_id=deep_peer(1)[0], device_id_type=MESH_ID,
        )

    def start_sum(slot):
        for k in range(1, 16):
            pltpu.make_async_remote_copy(
                src_ref=s_small.at[slot, 0], dst_ref=r_one.at[slot, p_me],
                send_sem=send_small.at[slot, 0], recv_sem=recv_small.at[slot, 0],
                device_id=wide_peer(k)[0], device_id_type=MESH_ID,
            ).start()
        r_one[slot, p_me] = s_small[slot, 0]

    def small_wait(slot, step, target, number):
        return pltpu.make_async_remote_copy(
            src_ref=target.at[slot, pl.ds(0, number - 1)], dst_ref=target.at[slot, pl.ds(0, number - 1)],
            send_sem=send_small.at[slot, step], recv_sem=recv_small.at[slot, step],
            device_id=deep_peer(1)[0], device_id_type=MESH_ID,
        )

    def middle_sum(slot):
        small_wait(slot, 0, r_one, 16).wait_recv()
        s_small[slot, 1] = jnp.sum(r_one[slot], axis=0)
        for k in range(1, 8):
            pltpu.make_async_remote_copy(
                src_ref=s_small.at[slot, 1], dst_ref=r_two.at[slot, q_me],
                send_sem=send_small.at[slot, 1], recv_sem=recv_small.at[slot, 1],
                device_id=deep_peer(k)[0], device_id_type=MESH_ID,
            ).start()
        r_two[slot, q_me] = s_small[slot, 1]

    def finish_sum(slot):
        small_wait(slot, 1, r_two, 8).wait_recv()
        return jnp.sum(r_two[slot], axis=0)

    def send_materials():
        material_copy.wait()
        for q in range(8):
            s_cell[q] = material[q].astype(F32).T.reshape(16, 8, N)
        me = xl_me * 8 + q_me
        for k in range(1, 16):
            device, xl, q = slab_peer(k)
            pltpu.make_async_remote_copy(
                src_ref=s_cell.at[q, xl * 8 + zb_me], dst_ref=r_cell.at[me],
                send_sem=cell_sem.at[0], recv_sem=cell_sem.at[1],
                device_id=device, device_id_type=MESH_ID,
            ).start()
        r_cell[me] = s_cell[q_me, p_me]

    cell_wait = pltpu.make_async_remote_copy(
        src_ref=r_cell.at[pl.ds(0, 15)], dst_ref=r_cell.at[pl.ds(0, 15)],
        send_sem=cell_sem.at[0], recv_sem=cell_sem.at[1],
        device_id=deep_peer(1)[0], device_id_type=MESH_ID,
    )

    def weigh_cells():
        cell_wait.wait_recv()
        kinds = jnp.dot(r_cell[...].reshape(N, N).astype(BF16), tab["order"][...], preferred_element_type=F32)
        met = (row // 8) == (lane // 8)
        placed = jnp.where(met, kinds, 0.0)
        for d in range(1, 16):
            moved = jnp.where(met, pltpu.roll(kinds, 8 * d, 1), 0.0)
            placed = placed + jnp.concatenate([moved[8 * d :], moved[: 8 * d]], 0)
        weights = jnp.zeros((N, N), F32)
        for kind in range(weight_ref.shape[0]):
            weights = weights + jnp.where(placed == float(kind), weight_ref[kind], 0.0)
        cell[...] = weights / CELLS

    def curl_and_send(kind, t, block):
        columns = []
        for c in range(3):
            halves = []
            for part in range(2):
                term = coef[c] * block[part]
                if c < 2:
                    term = term - coef[3 + c] * block[2 + part]
                halves.append(term)
            columns.append(jnp.concatenate(halves, 0))
        spread_x = rows_dot(tab["ta"], jnp.concatenate(columns, 1))
        op = kind // 4
        for c in range(3):
            s_a[op, t, :, c] = spread_x[:, c * N : (c + 1) * N].reshape(16, 2, 8, N)
        send(kind, t, s_a.at[op, t], r_a.at[op, t], wide_peer, 16, p_me)

    def z_stage(kind, t):
        op = kind // 4
        descriptor(kind - 1, t, s_a.at[op, t], r_a.at[op, t], 16).wait_recv()
        blocks = [r_a[op, t, pl.ds(xlo * 8, 8), c].reshape(N, N) for c in range(3) for xlo in range(2)]
        both = z_forward(tab, jnp.concatenate(blocks, 1))
        for k in range(6):
            for part in range(2):
                s_b[op, t, :, k, part] = both[k * 64 : (k + 1) * 64, part * N : (part + 1) * N].reshape(8, 8, N)
        send(kind, t, s_b.at[op, t], r_b.at[op, t], deep_peer, 8, q_me)

    def y_stage(kind, t):
        op = kind // 4
        descriptor(kind, t, s_b.at[op, t], r_b.at[op, t], 8).wait_recv()
        blocks = [r_b[op, t, :, pl.ds(2 * c, 2)].reshape(256, N) for c in range(3)]
        both = y_forward(tab, jnp.concatenate(blocks, 1))
        for c in range(3):
            for part in range(2):
                fields[t, c, part] = both[c * N : (c + 1) * N, part * N : (part + 1) * N].reshape(16, 8, N)

    def y_back_stage(t):
        weights = cell[...]
        rows = [
            jnp.concatenate([fields[t, c, part].reshape(N, N) * weights for part in range(2)], 1)
            for c in range(3)
        ]
        back = y_back(tab, jnp.concatenate(rows, 0))
        for c in range(3):
            s_c[t, :, pl.ds(2 * c, 2)] = back[:, c * N : (c + 1) * N].reshape(8, 2, 2, 8, N)
        send(2, t, s_c.at[t], r_c.at[t], deep_peer, 8, q_me)

    def z_back_stage(t):
        descriptor(2, t, s_c.at[t], r_c.at[t], 8).wait_recv()
        rows = [
            jnp.concatenate([r_c[t, :, k, part].reshape(64, N) for part in range(2)], 1) for k in range(6)
        ]
        back = z_back(tab, jnp.concatenate(rows, 0))
        for c in range(3):
            for xlo in range(2):
                k = 2 * c + xlo
                s_d[t, pl.ds(xlo * 8, 8), c] = back[:, k * N : (k + 1) * N].reshape(8, 2, 8, N)
        send(3, t, s_d.at[t], r_d.at[t], wide_peer, 16, p_me)

    def x_back_stage(t):
        descriptor(3, t, s_d.at[t], r_d.at[t], 16).wait_recv()
        columns = [r_d[t, :, c].reshape(256, N) for c in range(3)]
        back = rows_dot(tab["tat"], jnp.concatenate(columns, 1))
        for part in range(2):
            g = [back[part * N : (part + 1) * N, c * N : (c + 1) * N] for c in range(3)]
            image[t, 0, part] = (g[0] * coef[0] + g[1] * coef[1] + g[2] * coef[2]).reshape(16, 8, N)
            image[t, 1, part] = (-(g[0] * coef[3] + g[1] * coef[4])).reshape(16, 8, N)

    def gram(left, right, groups, slot, scale=None):
        def body(g, total):
            comp, m0 = g // 2, (g % 2) * 8
            left_cols = jnp.concatenate([left[:, comp, :, m0 + m].reshape(N, N) for m in range(8)], 1)
            if scale is None:
                right_cols = left_cols if right is left else jnp.concatenate(
                    [right[:, comp, :, m0 + m].reshape(N, N) for m in range(8)], 1
                )
            else:
                right_cols = []
                for m in range(8):
                    weight = scale[pl.ds(pl.multiple_of((m0 + m) * 8, 8), 8), :]
                    right_cols.append((right[:, comp, :, m0 + m] * weight[None, None]).reshape(N, N))
                right_cols = jnp.concatenate(right_cols, 1)
            lefts = jnp.concatenate(parts(left_cols), 0)
            rights = lefts if right_cols is left_cols else jnp.concatenate(parts(right_cols), 0)
            both = lax.dot_general(lefts, rights, (((1,), (1,)), ((), ())), preferred_element_type=F32)
            return total + (both[:N, :N] + ((both[:N, N:] + both[N:, :N]) + both[N:, N:]))

        total = lax.fori_loop(0, groups, body, jnp.zeros((N, N), F32))
        folded = exact_dot(tab["collect"][...], jnp.where(row % 8 == lane % 8, total, 0.0))
        sums = exact_dot(folded[:16], tab["place"][0]) + exact_dot(folded[16:], tab["place"][1])
        return pltpu.roll(sums, 16 * slot, 1) if slot else sums

    def mix():
        system = finish_sum(0)
        first_sum[...] = system
        rows16 = lax.broadcasted_iota(jnp.int32, (16, N), 0)
        for k in range(16):
            pivot = system[k : k + 1] / system[k : k + 1, k : k + 1]
            system = jnp.where(rows16 == k, pivot, system - system[:, k : k + 1] * pivot)
        wide = exact_dot(system, tab["spread"][...])
        spread_out = jnp.where(row % 8 == lane % 8, exact_dot(tab["gather"][...], wide).T, 0.0)
        mix_high, mix_low = parts(spread_out)
        mixing[:, :N] = mix_high
        mixing[:, N:] = mix_low

        def body(g, carry):
            comp, m0 = g // 2, (g % 2) * 8
            columns = jnp.concatenate([xt[:, comp, :, m0 + m].reshape(N, N) for m in range(8)], 1)
            mixed = rows_dot(mixing, columns)
            for m in range(8):
                search[:, comp, :, m0 + m] = mixed[:, m * N : (m + 1) * N].reshape(8, 2, 8, N)
            return carry

        lax.fori_loop(0, 4, body, 0)

    def out_copy(t):
        return pltpu.make_async_copy(out_stage.at[t], out_hbm.at[t], out_sem.at[t])

    def residual(t):
        block = []
        for comp in range(2):
            for part in range(2):
                left = (image[t, comp, part] - search[t, comp, part]).reshape(N, N) * coef[5]
                search[t, comp, part] = left.reshape(16, 8, N)
                block.append(left)
        curl_and_send(4, t, block)
        for comp in range(2):
            for part in range(2):
                out_stage[t, comp, part] = block[comp * 2 + part].T.reshape(16, 8, N)
        out_copy(t).start()

    def at(t, first, last, stage):
        @pl.when((t >= first) & (t < last))
        def _():
            stage()

    back, after = LAG_BACK, LAG_NEXT

    def step(t, carry):
        def load():
            band_copy(t).wait()
            for comp in range(2):
                for part in range(2):
                    xt[t, comp, part] = band_in[t, comp, part].reshape(N, N).T.reshape(16, 8, N)
            curl_and_send(0, t, [xt[t, c, r].reshape(N, N) for c in range(2) for r in range(2)])

        def rest_of_tables():
            for k in range(1, count):
                table_copy(k).wait()
            send_materials()

        def overlaps():
            s_small[0, 0] = gram(xt, xt, 4, 0)

        def overlaps_of_image():
            s_small[0, 0] = s_small[0, 0] + gram(fields, fields, 6, 1, cell)
            start_sum(0)

        def overlaps_of_search():
            s_small[1, 0] = gram(xt, search, 4, 0) + gram(search, search, 4, 1) + gram(search, image, 4, 2)

        at(t, 0, 8, load)
        at(t, 1, 2, rest_of_tables)
        at(t, 1, 9, lambda: z_stage(1, t - 1))
        at(t, back - 1, back, weigh_cells)
        at(t, back, back + 8, lambda: y_back_stage(t - back))
        at(t, back + 1, back + 9, lambda: z_back_stage(t - back - 1))
        at(t, 10, 11, lambda: middle_sum(0))
        at(t, back + 2, back + 10, lambda: x_back_stage(t - back - 2))
        at(t, after, after + 1, mix)
        at(t, after, after + 8, lambda: residual(t - after))
        at(t, after + 1, after + 9, lambda: z_stage(5, t - after - 1))
        at(t, 2, 10, lambda: y_stage(1, t - 2))
        at(t, 8, 9, overlaps)
        at(t, 9, 10, overlaps_of_image)
        at(t, after + 2, after + 10, lambda: y_stage(5, t - after - 2))
        at(t, after + 8, after + 9, overlaps_of_search)
        return carry

    lax.fori_loop(0, after + 10, step, 0)

    s_small[1, 0] = s_small[1, 0] + gram(fields, fields, 6, 3, cell)
    start_sum(1)
    middle_sum(1)
    second = finish_sum(1) / CELLS
    first = first_sum[...] / CELLS
    flipped = jnp.concatenate([second, jnp.zeros((N - 16, N), F32)], 0).T

    def joined(corner, right, below, last):
        return jnp.concatenate(
            [jnp.concatenate([corner, right], 1), jnp.concatenate([below, last], 1)], 0
        )

    corr_ref[0] = joined(first[:8, 0:8], second[:8, 0:8], flipped[0:8, :8], second[:8, 16:24])
    corr_ref[1] = joined(first[:8, 8:16], second[:8, 8:16], -flipped[8:16, :8], second[:8, 24:32])
    proj_ref[0] = joined(first[:8, 16:24], flipped[32:40, :8], second[:8, 32:40], second[:8, 48:56])
    proj_ref[1] = joined(first[:8, 24:32], -flipped[40:48, :8], second[:8, 40:48], second[:8, 56:64])

    def drain(t, carry):
        descriptor(0, t, s_a.at[0, t], r_a.at[0, t], 16).wait_send()
        descriptor(1, t, s_b.at[0, t], r_b.at[0, t], 8).wait_send()
        descriptor(2, t, s_c.at[t], r_c.at[t], 8).wait_send()
        descriptor(3, t, s_d.at[t], r_d.at[t], 16).wait_send()
        descriptor(4, t, s_a.at[1, t], r_a.at[1, t], 16).wait_send()
        descriptor(5, t, s_b.at[1, t], r_b.at[1, t], 8).wait_send()
        out_copy(t).wait()
        return carry

    lax.fori_loop(0, 8, drain, 0)
    cell_wait.wait_send()
    for slot in range(2):
        small_wait(slot, 0, r_one, 16).wait_send()
        small_wait(slot, 1, r_two, 8).wait_send()


def shards(band_block, material_grid, inverse_permittivity, bloch_index):
    table = {name: jnp.asarray(value) for name, value in tables().items()}
    vmem = pl.BlockSpec(memory_space=pltpu.VMEM)
    smem = pl.BlockSpec(memory_space=pltpu.SMEM)
    anywhere = pl.BlockSpec(memory_space=pl.ANY)
    block = (8, 2, 2, 16, 8, N)
    return pl.pallas_call(
        kernel,
        out_shape=(
            jax.ShapeDtypeStruct(band_block.shape, F32),
            jax.ShapeDtypeStruct((2, 16, 16), F32),
            jax.ShapeDtypeStruct((2, 16, 16), F32),
        ),
        in_specs=[smem, smem] + [anywhere] * (2 + len(NAMES)),
        out_specs=(anywhere, vmem, vmem),
        scratch_shapes=[
            pltpu.VMEM((6, N, N), F32),
            pltpu.VMEM(block, F32),
            pltpu.VMEM((8, N, N), jnp.int32),
            pltpu.VMEM((N, N), F32),
            pltpu.VMEM(block, F32),
            pltpu.VMEM(block, F32),
            pltpu.VMEM(block, F32),
            pltpu.VMEM(block, F32),
            pltpu.VMEM((8, 3, 2, 16, 8, N), F32),
            pltpu.VMEM((2, 8, 16, 3, 2, 8, N), F32),
            pltpu.VMEM((2, 8, 16, 3, 2, 8, N), F32),
            pltpu.VMEM((2, 8, 8, 6, 2, 8, N), F32),
            pltpu.VMEM((2, 8, 8, 6, 2, 8, N), F32),
            pltpu.VMEM((8, 8, 6, 2, 8, N), F32),
            pltpu.VMEM((8, 8, 6, 2, 8, N), F32),
            pltpu.VMEM((8, 16, 3, 2, 8, N), F32),
            pltpu.VMEM((8, 16, 3, 2, 8, N), F32),
            pltpu.VMEM((8, 16, 8, N), F32),
            pltpu.VMEM((16, 8, N), F32),
            pltpu.VMEM((2, 2, 16, N), F32),
            pltpu.VMEM((2, 16, 16, N), F32),
            pltpu.VMEM((2, 8, 16, N), F32),
            pltpu.VMEM((16, N), F32),
            pltpu.VMEM((N, 2 * N), BF16),
            pltpu.SemaphoreType.DMA((6, 8)),
            pltpu.SemaphoreType.DMA((6, 8)),
            pltpu.SemaphoreType.DMA((2, 2)),
            pltpu.SemaphoreType.DMA((2, 2)),
            pltpu.SemaphoreType.DMA((3,)),
            pltpu.SemaphoreType.DMA((8,)),
            pltpu.SemaphoreType.DMA((len(NAMES),)),
            pltpu.SemaphoreType.DMA((8,)),
        ] + [pltpu.VMEM(table[name].shape, table[name].dtype) for name in NAMES],
        compiler_params=pltpu.CompilerParams(
            collective_id=0, has_side_effects=True, vmem_limit_bytes=63 * 1024 * 1024
        ),
    )(bloch_index, inverse_permittivity, band_block, material_grid, *[table[name] for name in NAMES])


def solution(mesh):
    finer = Mesh(
        mesh.devices.reshape(4, 2, 2, 4, 2), ("band_0", "band_1", "slab_0", "slab_1", "slab_2")
    )
    placed = (P(None, None, None, BAND, SLAB, None), P(SLAB, None, None), P(), P())
    return jax.shard_map(
        shards,
        mesh=finer,
        in_specs=placed,
        out_specs=(P(None, None, None, BAND, SLAB, None), P(), P()),
        check_vma=False,
    )
```

time: 202 us -> 173 us (0.86)
  starting transfers between devices: 7.75 us -> 0 us
  local copies, waits for them, and re-layouts: 10.6 us -> 4.37 us
  waiting for transfers between devices: 5.17 us -> 0 us
  Pallas kernels: 172 us -> 167 us
  other arithmetic: 4.42 us -> 0 us
    all_to_all x1 -> x0, starting transfers between devices: 7.75 us -> none  [shards(): cells = lax.all_to_all(cells, SLAB, split_axis=0, concat_axis=0, tiled=True)]
    all_to_all x1 -> x0, waiting for transfers between devices: 5.17 us -> none  [shards(): cells = lax.all_to_all(cells, SLAB, split_axis=0, concat_axis=0, tiled=True)]
    pallas_call x1, Pallas kernels: 172 us -> 167 us  [shards(): pl.pallas_call(kernel, out_shape=(jax.ShapeDtypeStruct(band_block.shape,...]
    div x3 -> x0, other arithmetic: 3.41 us -> none  [the longest x1 2.71 us: shards(): cells = cells / CELLS]
    unnamed x6 -> x7, local copies, waits for them, and re-layouts: 5.26 us -> 4.37 us
  transfers between devices with their start and end apart: 1 -> 0, of which waited for: 1 -> 0; matrix products, arithmetic and copies ran while one was open for 0% -> 0% of each run, Pallas kernels for 0% -> 0%
where the time goes in v2:
time: 173 us
  Pallas kernels  167 us (97%)
  local copies, waits for them, and re-layouts  4.37 us (3%)
    pallas_call x1, Pallas kernels, shards(): pl.pallas_call(kernel, out_shape=(jax.ShapeDtypeStruct(band_block.shape,...  167 us
    unnamed x7, local copies, waits for them, and re-layouts  4.37 us

profile of v2, /device:TPU:1, one launch (start us, length us, event | category | flops | bytes accessed | tf_op | source)
XLA Modules:
  0.0 173.0 jit_solution(13480720760241846007)
XLA Ops:
  1.3 167.4 %shard_map.220 = (f32[8,2,2,16,8,128]{5,4,3,2,1,0:T(8,128)}, f32[2,16,16]{2,1,0:T(8,128)}, f32[2,16,16]{2,1,0:T(8,128)}) custom-call(s32[1]{0:T(128)S(6)} %copy.27.bloch_ref, f32[4]{0:T(128)} %weight_ref.1, f32[8,2,2,16,8,128]{5,4,3,2,1,0:T(8,128)} %band_hbm.1, s32[8,128,128]{2,1,0:T(8,128)} %material_hbm.1, bf16[256,512]{1,0:T(8,128)(2,1)} %constant.34.clone.refs_0_, ...), custom_call_target="tpu_custom_call" | custom-call | tf_op jit(solution)/shard_map/pallas_call | solution.py:553
  168.7 0.0 copy-start.1
  168.7 0.0 copy-start
  168.7 3.1 %copy.28 = f32[8,2,2,16,8,128]{5,4,3,2,1,0:T(8,128)} copy(f32[8,2,2,16,8,128]{5,4,3,2,1,0:T(8,128)} %get-tuple-element.6) | data formatting | bytes 4194304
  171.8 0.0 copy-done.1
  171.8 0.6 copy.29
  172.4 0.0 copy-done
  172.4 0.6 copy.30
Async XLA Ops:
  168.7 3.2 %copy-start.1 = (f32[2,16,16]{2,1,0:T(8,128)S(1)}, f32[2,16,16]{2,1,0:T(8,128)}, u32[]{:S(2)}) copy-start(f32[2,16,16]{2,1,0:T(8,128)} %get-tuple-element.7) | copy-start | bytes 6148
  168.7 3.8 %copy-start = (f32[2,16,16]{2,1,0:T(8,128)S(1)}, f32[2,16,16]{2,1,0:T(8,128)}, u32[]{:S(2)}) copy-start(f32[2,16,16]{2,1,0:T(8,128)} %get-tuple-element.8) | copy-start | bytes 6148

commit v3 on v2

--- a/solution.py
+++ b/solution.py
@@ -68,7 +68,7 @@
     turn[:8, 8:] = np.eye(8)
     turn[8:, :8] = -np.eye(8)
     turned = gather @ turn.T
-    collect = np.concatenate([gather.T, turned.T], 0)
+    collect = np.concatenate([gather.T[:8], turned.T[:8]], 0)
     place = np.zeros((2, 128, 128), np.float32)
     place[0, :, :16] = gather
     place[1, :, :16] = turned
@@ -174,8 +174,10 @@
     return 2.0 * math.pi / length * (signed + weight * fraction)
 
 
-LAG_BACK = 7
-LAG_NEXT = 11
+START = dict(A=(0, 2), B=(2, 1), C=(4, 1), Cb=(6, 1), Bb=(9, 1), Ab=(15, 2), R=(15, 2), B2=(17, 1), C2=(22, 1))
+ONCE = dict(cells=0, tables=1, gS=5, weigh=5, gH=12, m=13, mix=15, gJ1=21, gJ2=25, gJ3=23, gP=29)
+ORDER = ("B", "C2", "gJ1", "gP", "gJ2", "A", "cells", "tables", "B2", "gH", "Ab", "Bb", "gJ3", "m",
+         "weigh", "Cb", "mix", "gS", "R", "C")
 MESH_ID = pl.DeviceIdType.MESH
 
 
@@ -418,12 +420,15 @@
 
         total = lax.fori_loop(0, groups, body, jnp.zeros((N, N), F32))
         folded = exact_dot(tab["collect"][...], jnp.where(row % 8 == lane % 8, total, 0.0))
-        sums = exact_dot(folded[:16], tab["place"][0]) + exact_dot(folded[16:], tab["place"][1])
+        sums = exact_dot(folded[:8], tab["place"][0]) + exact_dot(folded[8:], tab["place"][1])
         return pltpu.roll(sums, 16 * slot, 1) if slot else sums
 
     def mix():
-        system = finish_sum(0)
-        first_sum[...] = system
+        top = finish_sum(0)
+        first_sum[...] = top
+        left = lax.broadcasted_iota(jnp.int32, (8, N), 1) % 16 < 8
+        below = jnp.where(left, -pltpu.roll(top, N - 8, 1), pltpu.roll(top, 8, 1))
+        system = jnp.concatenate([top, below], 0)
         rows16 = lax.broadcasted_iota(jnp.int32, (16, N), 0)
         for k in range(16):
             pivot = system[k : k + 1] / system[k : k + 1, k : k + 1]
@@ -460,62 +465,84 @@
                 out_stage[t, comp, part] = block[comp * 2 + part].T.reshape(16, 8, N)
         out_copy(t).start()
 
-    def at(t, first, last, stage):
-        @pl.when((t >= first) & (t < last))
+    def load(t):
+        band_copy(t).wait()
+        for comp in range(2):
+            for part in range(2):
+                xt[t, comp, part] = band_in[t, comp, part].reshape(N, N).T.reshape(16, 8, N)
+        curl_and_send(0, t, [xt[t, c, r].reshape(N, N) for c in range(2) for r in range(2)])
+
+    def rest_of_tables():
+        for k in range(1, count):
+            table_copy(k).wait()
+
+    def overlaps():
+        s_small[0, 0] = gram(xt, xt, 4, 0)
+
+    def overlaps_of_image():
+        s_small[0, 0] = s_small[0, 0] + gram(fields, fields, 6, 1, cell)
+        start_sum(0)
+
+    def first_overlaps_of_search():
+        s_small[1, 0] = gram(xt, search, 4, 0)
+
+    def add_overlaps(left, right, groups, slot, scale=None):
+        s_small[1, 0] = s_small[1, 0] + gram(left, right, groups, slot, scale)
+
+    stages = dict(
+        A=load,
+        B=lambda t: z_stage(1, t),
+        C=lambda t: y_stage(1, t),
+        Cb=y_back_stage,
+        Bb=z_back_stage,
+        Ab=x_back_stage,
+        R=residual,
+        B2=lambda t: z_stage(5, t),
+        C2=lambda t: y_stage(5, t),
+    )
+    once = dict(
+        cells=send_materials,
+        tables=rest_of_tables,
+        weigh=weigh_cells,
+        gS=overlaps,
+        gH=overlaps_of_image,
+        m=lambda: middle_sum(0),
+        mix=mix,
+        gJ1=first_overlaps_of_search,
+        gJ2=lambda: add_overlaps(search, search, 4, 1),
+        gJ3=lambda: add_overlaps(search, image, 4, 2),
+        gP=lambda: add_overlaps(fields, fields, 6, 3, cell),
+    )
+
+    def run(t, name):
+        if name in ONCE:
+            pl.when(t == ONCE[name])(once[name])
+            return
+        first, rate = START[name]
+
+        @pl.when((t >= first) & (t < first + 8 // rate))
         def _():
-            stage()
-
-    back, after = LAG_BACK, LAG_NEXT
+            if rate == 1:
+                stages[name](t - first)
+            else:
+                def body(k, carry):
+                    stages[name]((t - first) * rate + k)
+                    return carry
+
+                lax.fori_loop(0, rate, body, 0)
 
     def step(t, carry):
-        def load():
-            band_copy(t).wait()
-            for comp in range(2):
-                for part in range(2):
-                    xt[t, comp, part] = band_in[t, comp, part].reshape(N, N).T.reshape(16, 8, N)
-            curl_and_send(0, t, [xt[t, c, r].reshape(N, N) for c in range(2) for r in range(2)])
-
-        def rest_of_tables():
-            for k in range(1, count):
-                table_copy(k).wait()
-            send_materials()
-
-        def overlaps():
-            s_small[0, 0] = gram(xt, xt, 4, 0)
-
-        def overlaps_of_image():
-            s_small[0, 0] = s_small[0, 0] + gram(fields, fields, 6, 1, cell)
-            start_sum(0)
-
-        def overlaps_of_search():
-            s_small[1, 0] = gram(xt, search, 4, 0) + gram(search, search, 4, 1) + gram(search, image, 4, 2)
-
-        at(t, 0, 8, load)
-        at(t, 1, 2, rest_of_tables)
-        at(t, 1, 9, lambda: z_stage(1, t - 1))
-        at(t, back - 1, back, weigh_cells)
-        at(t, back, back + 8, lambda: y_back_stage(t - back))
-        at(t, back + 1, back + 9, lambda: z_back_stage(t - back - 1))
-        at(t, 10, 11, lambda: middle_sum(0))
-        at(t, back + 2, back + 10, lambda: x_back_stage(t - back - 2))
-        at(t, after, after + 1, mix)
-        at(t, after, after + 8, lambda: residual(t - after))
-        at(t, after + 1, after + 9, lambda: z_stage(5, t - after - 1))
-        at(t, 2, 10, lambda: y_stage(1, t - 2))
-        at(t, 8, 9, overlaps)
-        at(t, 9, 10, overlaps_of_image)
-        at(t, after + 2, after + 10, lambda: y_stage(5, t - after - 2))
-        at(t, after + 8, after + 9, overlaps_of_search)
+        for name in ORDER:
+            run(t, name)
         return carry
 
-    lax.fori_loop(0, after + 10, step, 0)
-
-    s_small[1, 0] = s_small[1, 0] + gram(fields, fields, 6, 3, cell)
+    lax.fori_loop(0, ONCE["gP"] + 1, step, 0)
+
     start_sum(1)
     middle_sum(1)
     second = finish_sum(1) / CELLS
     first = first_sum[...] / CELLS
-    flipped = jnp.concatenate([second, jnp.zeros((N - 16, N), F32)], 0).T
+    flipped = jnp.concatenate([second, jnp.zeros((N - 8, N), F32)], 0).T
 
     def joined(corner, right, below, last):
         return jnp.concatenate(
@@ -579,10 +606,10 @@
             pltpu.VMEM((8, 16, 3, 2, 8, N), F32),
             pltpu.VMEM((8, 16, 8, N), F32),
             pltpu.VMEM((16, 8, N), F32),
-            pltpu.VMEM((2, 2, 16, N), F32),
-            pltpu.VMEM((2, 16, 16, N), F32),
-            pltpu.VMEM((2, 8, 16, N), F32),
-            pltpu.VMEM((16, N), F32),
+            pltpu.VMEM((2, 2, 8, N), F32),
+            pltpu.VMEM((2, 16, 8, N), F32),
+            pltpu.VMEM((2, 8, 8, N), F32),
+            pltpu.VMEM((8, N), F32),
             pltpu.VMEM((N, 2 * N), BF16),
             pltpu.SemaphoreType.DMA((6, 8)),
             pltpu.SemaphoreType.DMA((6, 8)),

time: 173 us -> 165 us (0.954)
  Pallas kernels: 167 us -> 159 us
    pallas_call x1, Pallas kernels: 167 us -> 159 us  [shards(): pl.pallas_call(kernel, out_shape=(jax.ShapeDtypeStruct(band_block.shape,...]
where the time goes in v3:
time: 165 us
  Pallas kernels  159 us (96%)
  local copies, waits for them, and re-layouts  4.37 us (3%)
    pallas_call x1, Pallas kernels, shards(): pl.pallas_call(kernel, out_shape=(jax.ShapeDtypeStruct(band_block.shape,...  159 us
    unnamed x7, local copies, waits for them, and re-layouts  4.37 us

profile of v3, /device:TPU:1, one launch (start us, length us, event | category | flops | bytes accessed | tf_op | source)
XLA Modules:
  0.0 165.1 jit_solution(13219961559189740445)
XLA Ops:
  1.3 159.4 %shard_map.220 = (f32[8,2,2,16,8,128]{5,4,3,2,1,0:T(8,128)}, f32[2,16,16]{2,1,0:T(8,128)}, f32[2,16,16]{2,1,0:T(8,128)}) custom-call(s32[1]{0:T(128)S(6)} %copy.27.bloch_ref, f32[4]{0:T(128)} %weight_ref.1, f32[8,2,2,16,8,128]{5,4,3,2,1,0:T(8,128)} %band_hbm.1, s32[8,128,128]{2,1,0:T(8,128)} %material_hbm.1, bf16[256,512]{1,0:T(8,128)(2,1)} %constant.34.clone.refs_0_, ...), custom_call_target="tpu_custom_call" | custom-call | tf_op jit(solution)/shard_map/pallas_call | solution.py:580
  160.7 0.0 copy-start.1
  160.7 0.0 copy-start
  160.7 3.1 %copy.28 = f32[8,2,2,16,8,128]{5,4,3,2,1,0:T(8,128)} copy(f32[8,2,2,16,8,128]{5,4,3,2,1,0:T(8,128)} %get-tuple-element.6) | data formatting | bytes 4194304
  163.9 0.0 copy-done.1
  163.9 0.6 copy.29
  164.5 0.0 copy-done
  164.5 0.6 copy.30
Async XLA Ops:
  160.7 3.2 %copy-start.1 = (f32[2,16,16]{2,1,0:T(8,128)S(1)}, f32[2,16,16]{2,1,0:T(8,128)}, u32[]{:S(2)}) copy-start(f32[2,16,16]{2,1,0:T(8,128)} %get-tuple-element.7) | copy-start | bytes 6148
  160.7 3.8 %copy-start = (f32[2,16,16]{2,1,0:T(8,128)S(1)}, f32[2,16,16]{2,1,0:T(8,128)}, u32[]{:S(2)}) copy-start(f32[2,16,16]{2,1,0:T(8,128)} %get-tuple-element.8) | copy-start | bytes 6148

commit v4 on v3

--- a/solution.py
+++ b/solution.py
@@ -47,12 +47,8 @@
     i128, i16, i8 = np.arange(128), np.arange(16), np.arange(8)
     r = _rot(tau / 128 * (i128[:, None] * i128[None, :] % 128))
     ta = r.reshape(2, 2, 16, 8, 128).transpose(2, 0, 3, 1, 4).reshape(256, 256)
-    r = _rot(tau / 8 * (i8[:, None] * i8[None, :] % 8))
-    kz = np.einsum("abzs,xy->azxsby", r, np.eye(8)).reshape(128, 128)
     r = _rot(tau / 16 * (i16[:, None] * i16[None, :] % 16))
     wz = np.einsum("abos,xy->bsxaoy", r, np.eye(8)).reshape(256, 256)
-    r = _rot(tau / 16 * (i16[:, None] * i16[None, :] % 16)).reshape(2, 2, 16, 2, 8)
-    ky = np.einsum("abolq,xy->aoxqlby", r, np.eye(8)).reshape(256, 256)
     r = _rot(tau / 8 * (i8[:, None] * i8[None, :] % 8))
     wy = np.einsum("abos,xy->bxsayo", r, np.eye(16)).reshape(256, 256)
     lane = np.arange(128)
@@ -77,13 +73,13 @@
     order = np.zeros((128, 128), np.float32)
     order[lane, lane % 16 * 8 + lane // 16] = 1.0
     return dict(
-        ta=_left(ta), tat=_left(ta.T), kz=_left(kz), kzt=_left(kz.T), ky=_left(ky), kyt=_left(ky.T),
+        ta=_left(ta), tat=_left(ta.T),
         wz=_right(wz), wzt=_right(wz.T), wy=_right(wy), wyt=_right(wy.T),
         twz=twz, twy=twy, collect=collect, place=place, spread=spread, gather=gather, order=order.astype(BF16),
     )
 
 
-NAMES = ("ta", "tat", "kz", "kzt", "ky", "kyt", "wz", "wzt", "wy", "wyt", "twz", "twy",
+NAMES = ("ta", "tat", "wz", "wzt", "wy", "wyt", "twz", "twy",
          "collect", "place", "spread", "gather", "order")
 
 
@@ -125,48 +121,47 @@
     return re * cosine + im * sine, im * cosine - re * sine
 
 
-def cut(x, size, axis=1):
-    return [lax.slice_in_dim(x, k, k + size, axis=axis) for k in range(0, x.shape[axis], size)]
-
-
-def z_forward(tab, blocks):
-    mixed = rows_dot(tab["kz"], blocks)
-    cosine, sine = tab["twz"][0], tab["twz"][1]
-    pairs = [turn_by(b[:64], b[64:], cosine, sine) for b in cut(mixed, 128)]
-    both = jnp.concatenate(
-        [jnp.concatenate([a for a, _ in pairs], 0), jnp.concatenate([b for _, b in pairs], 0)], 1
-    )
-    return lanes_dot(both, tab["wz"])
-
-
-def z_back(tab, both):
-    mixed = lanes_dot(both, tab["wzt"])
-    cosine, sine = tab["twz"][0], tab["twz"][1]
-    blocks = []
-    for b in cut(mixed, 64, 0):
-        re, im = turn_back(b[:, :128], b[:, 128:], cosine, sine)
-        blocks.append(jnp.concatenate([re, im], 0))
-    return rows_dot(tab["kzt"], jnp.concatenate(blocks, 1))
-
-
-def y_forward(tab, blocks):
-    mixed = rows_dot(tab["ky"], blocks)
-    cosine, sine = tab["twy"][0], tab["twy"][1]
-    pairs = [turn_by(b[:128], b[128:], cosine, sine) for b in cut(mixed, 128)]
-    both = jnp.concatenate(
-        [jnp.concatenate([a for a, _ in pairs], 0), jnp.concatenate([b for _, b in pairs], 0)], 1
-    )
-    return lanes_dot(both, tab["wy"])
-
-
-def y_back(tab, both):
-    mixed = lanes_dot(both, tab["wyt"])
-    cosine, sine = tab["twy"][0], tab["twy"][1]
-    blocks = []
-    for b in cut(mixed, 128, 0):
-        re, im = turn_back(b[:, :128], b[:, 128:], cosine, sine)
-        blocks.append(jnp.concatenate([re, im], 0))
-    return rows_dot(tab["kyt"], jnp.concatenate(blocks, 1))
+def times_root(value, k, n, sign):
+    re, im = value
+    if k == 0:
+        return value
+    if 4 * k == n:
+        return (-im, re) if sign > 0 else (im, -re)
+    cosine, sine = math.cos(2.0 * math.pi * k / n), sign * math.sin(2.0 * math.pi * k / n)
+    if 8 * k == n:
+        return ((re - im) * cosine, (re + im) * cosine) if sign > 0 else ((re + im) * cosine, (im - re) * cosine)
+    return re * cosine - im * sine, re * sine + im * cosine
+
+
+def short_transform(values, sign):
+    n = len(values)
+    if n == 1:
+        return values
+    even, odd = short_transform(values[0::2], sign), short_transform(values[1::2], sign)
+    turned = [times_root(odd[k], k, n, sign) for k in range(n // 2)]
+    return [(even[k][0] + turned[k][0], even[k][1] + turned[k][1]) for k in range(n // 2)] + [
+        (even[k][0] - turned[k][0], even[k][1] - turned[k][1]) for k in range(n // 2)
+    ]
+
+
+def rows_of(values):
+    return jnp.concatenate(
+        [jnp.concatenate([v[0] for v in values], 0), jnp.concatenate([v[1] for v in values], 0)], 1
+    )
+
+
+def twisted(values, twist, turn):
+    return values[:1] + [
+        turn(v[0], v[1], twist[0, 8 * k : 8 * k + 8], twist[1, 8 * k : 8 * k + 8])
+        for k, v in enumerate(values)
+        if k
+    ]
+
+
+def tiles_of(both, start, number):
+    return [
+        (both[8 * k : 8 * k + 8, :128], both[8 * k : 8 * k + 8, 128:]) for k in range(start, start + number)
+    ]
 
 
 def axis_values(length, weight, fraction, indices):
@@ -174,17 +169,19 @@
     return 2.0 * math.pi / length * (signed + weight * fraction)
 
 
-START = dict(A=(0, 2), B=(2, 1), C=(4, 1), Cb=(6, 1), Bb=(9, 1), Ab=(15, 2), R=(15, 2), B2=(17, 1), C2=(22, 1))
-ONCE = dict(cells=0, tables=1, gS=5, weigh=5, gH=12, m=13, mix=15, gJ1=21, gJ2=25, gJ3=23, gP=29)
-ORDER = ("B", "C2", "gJ1", "gP", "gJ2", "A", "cells", "tables", "B2", "gH", "Ab", "Bb", "gJ3", "m",
-         "weigh", "Cb", "mix", "gS", "R", "C")
+RATE = dict(A=(0, 2, 1), B=(2, 4, 1), C=(4, 4, 1), Cb=(7, 3, 1), Bb=(8, 2, 1), Ab=(14, 2, 3), R=(19, 2, 3), B2=(24, 2,
+    1), C2=(27, 2, 1))
+ONCE = dict(cells=0, tables=0, weigh=5, gS=8, gH=10, m=12, mix=17, gJ1=32, gJ2=37, gJ3=34, gP=38)
+ORDER = ("R", "gJ2", "gH", "Ab", "weigh", "gJ1", "mix", "Cb", "B", "m", "C", "C2", "A", "cells", "tables", "gP", "gS",
+    "Bb", "B2", "gJ3")
+CHUNKED = ("B", "C", "Cb", "Bb", "B2", "C2")
 MESH_ID = pl.DeviceIdType.MESH
 
 
 def kernel(bloch_ref, weight_ref, band_hbm, material_hbm, *refs):
     count = len(NAMES)
     table_hbm = refs[:count]
-    (out_hbm, corr_ref, proj_ref, coef, band_in, material, cell, xt, image, search, out_stage, fields,
+    (out_hbm, corr_ref, proj_ref, coef, band_in, material, cell, xt, image, search, fields,
      s_a, r_a, s_b, r_b, s_c, r_c, s_d, r_d, s_cell, r_cell, s_small, r_one, r_two, first_sum, mixing,
      send_x, recv_x, send_small, recv_small, cell_sem, in_sem, table_sem, out_sem) = refs[count : -count]
     tab = dict(zip(NAMES, refs[-count:]))
@@ -345,54 +342,65 @@
         spread_x = rows_dot(tab["ta"], jnp.concatenate(columns, 1))
         op = kind // 4
         for c in range(3):
-            s_a[op, t, :, c] = spread_x[:, c * N : (c + 1) * N].reshape(16, 2, 8, N)
-        send(kind, t, s_a.at[op, t], r_a.at[op, t], wide_peer, 16, p_me)
-
-    def z_stage(kind, t):
+            s_a[op, 3 * t + c] = spread_x[:, c * N : (c + 1) * N].reshape(16, 2, 8, N)
+
+        def body(c, carry):
+            k = 3 * t + c
+            send(kind, k, s_a.at[op, k], r_a.at[op, k], wide_peer, 16, p_me)
+            return carry
+
+        lax.fori_loop(0, 3, body, 0)
+
+    def z_stage(kind, k):
         op = kind // 4
-        descriptor(kind - 1, t, s_a.at[op, t], r_a.at[op, t], 16).wait_recv()
-        blocks = [r_a[op, t, pl.ds(xlo * 8, 8), c].reshape(N, N) for c in range(3) for xlo in range(2)]
-        both = z_forward(tab, jnp.concatenate(blocks, 1))
-        for k in range(6):
+        descriptor(kind - 1, k, s_a.at[op, k], r_a.at[op, k], 16).wait_recv()
+        values = []
+        for xlo in range(2):
+            arrived = [(r_a[op, k, xlo * 8 + z, 0], r_a[op, k, xlo * 8 + z, 1]) for z in range(8)]
+            values += twisted(short_transform(arrived, 1), tab["twz"], turn_by)
+        both = lanes_dot(rows_of(values), tab["wz"])
+        for xlo in range(2):
             for part in range(2):
-                s_b[op, t, :, k, part] = both[k * 64 : (k + 1) * 64, part * N : (part + 1) * N].reshape(8, 8, N)
-        send(kind, t, s_b.at[op, t], r_b.at[op, t], deep_peer, 8, q_me)
-
-    def y_stage(kind, t):
+                s_b[op, k, :, xlo, part] = both[xlo * 64 : (xlo + 1) * 64, part * N : (part + 1) * N].reshape(8, 8, N)
+        send(kind, k, s_b.at[op, k], r_b.at[op, k], deep_peer, 8, q_me)
+
+    def y_stage(kind, k):
         op = kind // 4
-        descriptor(kind, t, s_b.at[op, t], r_b.at[op, t], 8).wait_recv()
-        blocks = [r_b[op, t, :, pl.ds(2 * c, 2)].reshape(256, N) for c in range(3)]
-        both = y_forward(tab, jnp.concatenate(blocks, 1))
+        descriptor(kind, k, s_b.at[op, k], r_b.at[op, k], 8).wait_recv()
+        arrived = [(r_b[op, k, y % 8, y // 8, 0], r_b[op, k, y % 8, y // 8, 1]) for y in range(16)]
+        values = twisted(short_transform(arrived, 1), tab["twy"], turn_by)
+        both = lanes_dot(rows_of(values), tab["wy"])
+        for part in range(2):
+            fields[k // 3, k % 3, part] = both[:, part * N : (part + 1) * N].reshape(16, 8, N)
+
+    def y_back_stage(k):
+        weights = cell[...]
+        both = jnp.concatenate([fields[k // 3, k % 3, part].reshape(N, N) * weights for part in range(2)], 1)
+        mixed = tiles_of(lanes_dot(both, tab["wyt"]), 0, 16)
+        for y, (re, im) in enumerate(short_transform(twisted(mixed, tab["twy"], turn_back), -1)):
+            s_c[k, y % 8, y // 8, 0] = re
+            s_c[k, y % 8, y // 8, 1] = im
+        send(2, k, s_c.at[k], r_c.at[k], deep_peer, 8, q_me)
+
+    def z_back_stage(k):
+        descriptor(2, k, s_c.at[k], r_c.at[k], 8).wait_recv()
+        rows = [
+            jnp.concatenate([r_c[k, :, xlo, part].reshape(64, N) for part in range(2)], 1) for xlo in range(2)
+        ]
+        both = lanes_dot(jnp.concatenate(rows, 0), tab["wzt"])
+        for xlo in range(2):
+            mixed = twisted(tiles_of(both, xlo * 8, 8), tab["twz"], turn_back)
+            for z, (re, im) in enumerate(short_transform(mixed, -1)):
+                s_d[k, xlo * 8 + z, 0] = re
+                s_d[k, xlo * 8 + z, 1] = im
+        send(3, k, s_d.at[k], r_d.at[k], wide_peer, 16, p_me)
+
+    def x_back_stage(t):
+        columns = []
         for c in range(3):
-            for part in range(2):
-                fields[t, c, part] = both[c * N : (c + 1) * N, part * N : (part + 1) * N].reshape(16, 8, N)
-
-    def y_back_stage(t):
-        weights = cell[...]
-        rows = [
-            jnp.concatenate([fields[t, c, part].reshape(N, N) * weights for part in range(2)], 1)
-            for c in range(3)
-        ]
-        back = y_back(tab, jnp.concatenate(rows, 0))
-        for c in range(3):
-            s_c[t, :, pl.ds(2 * c, 2)] = back[:, c * N : (c + 1) * N].reshape(8, 2, 2, 8, N)
-        send(2, t, s_c.at[t], r_c.at[t], deep_peer, 8, q_me)
-
-    def z_back_stage(t):
-        descriptor(2, t, s_c.at[t], r_c.at[t], 8).wait_recv()
-        rows = [
-            jnp.concatenate([r_c[t, :, k, part].reshape(64, N) for part in range(2)], 1) for k in range(6)
-        ]
-        back = z_back(tab, jnp.concatenate(rows, 0))
-        for c in range(3):
-            for xlo in range(2):
-                k = 2 * c + xlo
-                s_d[t, pl.ds(xlo * 8, 8), c] = back[:, k * N : (k + 1) * N].reshape(8, 2, 8, N)
-        send(3, t, s_d.at[t], r_d.at[t], wide_peer, 16, p_me)
-
-    def x_back_stage(t):
-        descriptor(3, t, s_d.at[t], r_d.at[t], 16).wait_recv()
-        columns = [r_d[t, :, c].reshape(256, N) for c in range(3)]
+            k = 3 * t + c
+            descriptor(3, k, s_d.at[k], r_d.at[k], 16).wait_recv()
+            columns.append(r_d[k].reshape(256, N))
         back = rows_dot(tab["tat"], jnp.concatenate(columns, 1))
         for part in range(2):
             g = [back[part * N : (part + 1) * N, c * N : (c + 1) * N] for c in range(3)]
@@ -450,7 +458,7 @@
         lax.fori_loop(0, 4, body, 0)
 
     def out_copy(t):
-        return pltpu.make_async_copy(out_stage.at[t], out_hbm.at[t], out_sem.at[t])
+        return pltpu.make_async_copy(band_in.at[t], out_hbm.at[t], out_sem.at[t])
 
     def residual(t):
         block = []
@@ -462,7 +470,7 @@
         curl_and_send(4, t, block)
         for comp in range(2):
             for part in range(2):
-                out_stage[t, comp, part] = block[comp * 2 + part].T.reshape(16, 8, N)
+                band_in[t, comp, part] = block[comp * 2 + part].T.reshape(16, 8, N)
         out_copy(t).start()
 
     def load(t):
@@ -518,18 +526,17 @@
         if name in ONCE:
             pl.when(t == ONCE[name])(once[name])
             return
-        first, rate = START[name]
-
-        @pl.when((t >= first) & (t < first + 8 // rate))
+        first, count_of, per = RATE[name]
+        total = 24 if name in CHUNKED else 8
+
+        def body(k, carry):
+            stages[name](k)
+            return carry
+
+        @pl.when((t >= first) & (t <= first + (total * per - 1) // count_of))
         def _():
-            if rate == 1:
-                stages[name](t - first)
-            else:
-                def body(k, carry):
-                    stages[name]((t - first) * rate + k)
-                    return carry
-
-                lax.fori_loop(0, rate, body, 0)
+            since = t - first
+            lax.fori_loop(since * count_of // per, jnp.minimum((since + 1) * count_of // per, total), body, 0)
 
     def step(t, carry):
         for name in ORDER:
@@ -561,10 +568,11 @@
         descriptor(3, t, s_d.at[t], r_d.at[t], 16).wait_send()
         descriptor(4, t, s_a.at[1, t], r_a.at[1, t], 16).wait_send()
         descriptor(5, t, s_b.at[1, t], r_b.at[1, t], 8).wait_send()
+        return carry
+
+    lax.fori_loop(0, 24, drain, 0)
+    for t in range(8):
         out_copy(t).wait()
-        return carry
-
-    lax.fori_loop(0, 8, drain, 0)
     cell_wait.wait_send()
     for slot in range(2):
         small_wait(slot, 0, r_one, 16).wait_send()
@@ -594,16 +602,15 @@
             pltpu.VMEM(block, F32),
             pltpu.VMEM(block, F32),
             pltpu.VMEM(block, F32),
-            pltpu.VMEM(block, F32),
             pltpu.VMEM((8, 3, 2, 16, 8, N), F32),
-            pltpu.VMEM((2, 8, 16, 3, 2, 8, N), F32),
-            pltpu.VMEM((2, 8, 16, 3, 2, 8, N), F32),
-            pltpu.VMEM((2, 8, 8, 6, 2, 8, N), F32),
-            pltpu.VMEM((2, 8, 8, 6, 2, 8, N), F32),
-            pltpu.VMEM((8, 8, 6, 2, 8, N), F32),
-            pltpu.VMEM((8, 8, 6, 2, 8, N), F32),
-            pltpu.VMEM((8, 16, 3, 2, 8, N), F32),
-            pltpu.VMEM((8, 16, 3, 2, 8, N), F32),
+            pltpu.VMEM((2, 24, 16, 2, 8, N), F32),
+            pltpu.VMEM((2, 24, 16, 2, 8, N), F32),
+            pltpu.VMEM((2, 24, 8, 2, 2, 8, N), F32),
+            pltpu.VMEM((2, 24, 8, 2, 2, 8, N), F32),
+            pltpu.VMEM((24, 8, 2, 2, 8, N), F32),
+            pltpu.VMEM((24, 8, 2, 2, 8, N), F32),
+            pltpu.VMEM((24, 16, 2, 8, N), F32),
+            pltpu.VMEM((24, 16, 2, 8, N), F32),
             pltpu.VMEM((8, 16, 8, N), F32),
             pltpu.VMEM((16, 8, N), F32),
             pltpu.VMEM((2, 2, 8, N), F32),
@@ -611,8 +618,8 @@
             pltpu.VMEM((2, 8, 8, N), F32),
             pltpu.VMEM((8, N), F32),
             pltpu.VMEM((N, 2 * N), BF16),
-            pltpu.SemaphoreType.DMA((6, 8)),
-            pltpu.SemaphoreType.DMA((6, 8)),
+            pltpu.SemaphoreType.DMA((6, 24)),
+            pltpu.SemaphoreType.DMA((6, 24)),
             pltpu.SemaphoreType.DMA((2, 2)),
             pltpu.SemaphoreType.DMA((2, 2)),
             pltpu.SemaphoreType.DMA((3,)),

time: 165 us -> 155 us (0.939)
  Pallas kernels: 159 us -> 149 us
    pallas_call x1, Pallas kernels: 159 us -> 149 us  [shards(): pl.pallas_call(kernel, out_shape=(jax.ShapeDtypeStruct(band_block.shape,...]
where the time goes in v4:
time: 155 us
  Pallas kernels  149 us (96%)
  local copies, waits for them, and re-layouts  4.37 us (3%)
    pallas_call x1, Pallas kernels, shards(): pl.pallas_call(kernel, out_shape=(jax.ShapeDtypeStruct(band_block.shape,...  149 us
    unnamed x7, local copies, waits for them, and re-layouts  4.37 us

profile of v4, /device:TPU:1, one launch (start us, length us, event | category | flops | bytes accessed | tf_op | source)
XLA Modules:
  0.0 155.0 jit_solution(43935488224037046)
XLA Ops:
  1.3 149.4 %shard_map.184 = (f32[8,2,2,16,8,128]{5,4,3,2,1,0:T(8,128)}, f32[2,16,16]{2,1,0:T(8,128)}, f32[2,16,16]{2,1,0:T(8,128)}) custom-call(s32[1]{0:T(128)S(6)} %copy.23.bloch_ref, f32[4]{0:T(128)} %weight_ref.1, f32[8,2,2,16,8,128]{5,4,3,2,1,0:T(8,128)} %band_hbm.1, s32[8,128,128]{2,1,0:T(8,128)} %material_hbm.1, bf16[256,512]{1,0:T(8,128)(2,1)} %constant.26.clone.refs_0_, ...), custom_call_target="tpu_custom_call" | custom-call | tf_op jit(solution)/shard_map/pallas_call | solution.py:588
  150.6 0.0 copy-start.1
  150.7 0.0 copy-start
  150.7 3.1 %copy.24 = f32[8,2,2,16,8,128]{5,4,3,2,1,0:T(8,128)} copy(f32[8,2,2,16,8,128]{5,4,3,2,1,0:T(8,128)} %get-tuple-element.6) | data formatting | bytes 4194304
  153.8 0.0 copy-done.1
  153.8 0.6 copy.25
  154.4 0.0 copy-done
  154.4 0.6 copy.26
Async XLA Ops:
  150.6 3.2 %copy-start.1 = (f32[2,16,16]{2,1,0:T(8,128)S(1)}, f32[2,16,16]{2,1,0:T(8,128)}, u32[]{:S(2)}) copy-start(f32[2,16,16]{2,1,0:T(8,128)} %get-tuple-element.7) | copy-start | bytes 6148
  150.7 3.8 %copy-start = (f32[2,16,16]{2,1,0:T(8,128)S(1)}, f32[2,16,16]{2,1,0:T(8,128)}, u32[]{:S(2)}) copy-start(f32[2,16,16]{2,1,0:T(8,128)} %get-tuple-element.8) | copy-start | bytes 6148

commit v5 on v4

--- a/solution.py
+++ b/solution.py
@@ -181,9 +181,9 @@
 def kernel(bloch_ref, weight_ref, band_hbm, material_hbm, *refs):
     count = len(NAMES)
     table_hbm = refs[:count]
-    (out_hbm, corr_ref, proj_ref, coef, band_in, material, cell, xt, image, search, fields,
+    (out_ref, corr_ref, proj_ref, coef, band_in, material, cell, xt, image, search, fields,
      s_a, r_a, s_b, r_b, s_c, r_c, s_d, r_d, s_cell, r_cell, s_small, r_one, r_two, first_sum, mixing,
-     send_x, recv_x, send_small, recv_small, cell_sem, in_sem, table_sem, out_sem) = refs[count : -count]
+     send_x, recv_x, send_small, recv_small, cell_sem, in_sem, table_sem) = refs[count : -count]
     tab = dict(zip(NAMES, refs[-count:]))
     y_me, xh_me, xl_me = (lax.axis_index(a) for a in ("band_0", "band_1", "slab_0"))
     z_me, c_me = lax.axis_index("slab_1"), lax.axis_index("slab_2")
@@ -457,9 +457,6 @@
 
         lax.fori_loop(0, 4, body, 0)
 
-    def out_copy(t):
-        return pltpu.make_async_copy(band_in.at[t], out_hbm.at[t], out_sem.at[t])
-
     def residual(t):
         block = []
         for comp in range(2):
@@ -470,8 +467,7 @@
         curl_and_send(4, t, block)
         for comp in range(2):
             for part in range(2):
-                band_in[t, comp, part] = block[comp * 2 + part].T.reshape(16, 8, N)
-        out_copy(t).start()
+                out_ref[t, comp, part] = block[comp * 2 + part].T.reshape(16, 8, N)
 
     def load(t):
         band_copy(t).wait()
@@ -571,8 +567,6 @@
         return carry
 
     lax.fori_loop(0, 24, drain, 0)
-    for t in range(8):
-        out_copy(t).wait()
     cell_wait.wait_send()
     for slot in range(2):
         small_wait(slot, 0, r_one, 16).wait_send()
@@ -588,12 +582,12 @@
     return pl.pallas_call(
         kernel,
         out_shape=(
-            jax.ShapeDtypeStruct(band_block.shape, F32),
-            jax.ShapeDtypeStruct((2, 16, 16), F32),
-            jax.ShapeDtypeStruct((2, 16, 16), F32),
+            pltpu.VMEM(band_block.shape, F32),
+            pltpu.VMEM((2, 16, 16), F32),
+            pltpu.VMEM((2, 16, 16), F32),
         ),
         in_specs=[smem, smem] + [anywhere] * (2 + len(NAMES)),
-        out_specs=(anywhere, vmem, vmem),
+        out_specs=(vmem, vmem, vmem),
         scratch_shapes=[
             pltpu.VMEM((6, N, N), F32),
             pltpu.VMEM(block, F32),
@@ -625,10 +619,9 @@
             pltpu.SemaphoreType.DMA((3,)),
             pltpu.SemaphoreType.DMA((8,)),
             pltpu.SemaphoreType.DMA((len(NAMES),)),
-            pltpu.SemaphoreType.DMA((8,)),
         ] + [pltpu.VMEM(table[name].shape, table[name].dtype) for name in NAMES],
         compiler_params=pltpu.CompilerParams(
-            collective_id=0, has_side_effects=True, vmem_limit_bytes=63 * 1024 * 1024
+            collective_id=0, has_side_effects=True, vmem_limit_bytes=58 * 1024 * 1024
         ),
     )(bloch_index, inverse_permittivity, band_block, material_grid, *[table[name] for name in NAMES])
 

time: 155 us -> 153 us (0.987)
  local copies, waits for them, and re-layouts: 4.37 us -> 2.53 us
    unnamed x7 -> x3, local copies, waits for them, and re-layouts: 4.37 us -> 2.53 us
where the time goes in v5:
time: 153 us; the launch traced here: 152 us
  Pallas kernels  149 us (97%)
  local copies, waits for them, and re-layouts  2.53 us (2%)
    pallas_call x1, Pallas kernels, shards(): pl.pallas_call(kernel, out_shape=(pltpu.VMEM(band_block.shape, F32), pltp...  149 us

profile of v5, /device:TPU:1, one launch (start us, length us, event | category | flops | bytes accessed | tf_op | source)
XLA Modules:
  0.0 152.5 jit_solution(4221077054026272754)
XLA Ops:
  1.3 148.7 %shard_map.184 = (f32[8,2,2,16,8,128]{5,4,3,2,1,0:T(8,128)S(1)}, f32[2,16,16]{2,1,0:T(8,128)S(1)}, f32[2,16,16]{2,1,0:T(8,128)S(1)}) custom-call(s32[1]{0:T(128)S(6)} %copy.26.bloch_ref, f32[4]{0:T(128)} %weight_ref.1, f32[8,2,2,16,8,128]{5,4,3,2,1,0:T(8,128)} %band_hbm.1, s32[8,128,128]{2,1,0:T(8,128)} %material_hbm.1, ...), custom_call_target="tpu_custom_call" | custom-call | tf_op jit(solution)/shard_map/pallas_call | solution.py:582
  150.0 1.3 copy.23
  151.3 0.6 copy.24
  151.9 0.6 copy.25
